TPU v7x, 32 devices: a whole 2x2x4 slice. The times are simulated.
32 devices in a mesh: slab: 4 (over z), tile: 8 (over y, x, core).
Axes of the slice: x: 2, y: 2, z: 4, core: 2. Of those that a mesh axis runs over, the one named last changes fastest.
Arguments:
- voxel_grid: float32 [4, 64, 64, 256], P(None, 'slab', 'tile'), may hold values from -4 to 4
- first_moment: float32 [4, 64, 64, 256], P(None, 'slab', 'tile'), may hold values from -0.75 to 0.75
- second_moment: float32 [4, 64, 64, 256], P(None, 'slab', 'tile'), may hold values from 0.01 to 0.5
- pixel_index: int32 [32768], P('tile'), may hold values from 0 to 2047
- start_slab: int32 [32768], P('tile'), may hold values from 0 to 1
- ray_count: int32 [32768], P('tile'), may hold values from 16 to 48
- target: float32 [3, 32768], P(None, 'tile'), may hold values from 0 to 1
Outputs:
- new_grid: float32 [4, 64, 64, 256], P(None, 'slab', 'tile')
- new_first: float32 [4, 64, 64, 256], P(None, 'slab', 'tile')
- new_second: float32 [4, 64, 64, 256], P(None, 'slab', 'tile')
All inputs are finite; a program needn't handle non-finite values.
Results may differ from a plain program's by a relative error of at most 0.0003.
Values sent between devices are 32-bit elements; how exact they have to be, the bound alone decides.
A program may use at most 128 MiB of HBM per device.

v0:
```python
import functools
import math

import jax
import jax.numpy as jnp
from jax import lax
from jax.experimental import pallas as pl
from jax.experimental.pallas import tpu as pltpu
from jax.sharding import PartitionSpec as P

STEP = 20
RENDER_WEIGHT = 1000.0
TV_WEIGHT = 0.05
BACKGROUND = 1.0
STEP_SPAN = 4.0
CLIP_RMS = 0.25
LEARN_RATE = 0.02
BETA_ONE = 0.9
BETA_TWO = 0.99
EPSILON = 1e-08
CHUNK = 512
DIRECT_LIMIT = 64
MESH = pl.DeviceIdType.MESH


def kernel(
    ns, nt, chunk,
    grid_hbm, first_hbm, second_hbm, pix_hbm, start_hbm, count_hbm, target_hbm,
    grid_ref, first_ref, second_ref, grad_ref, scale_ref,
    pix_ref, start_ref, count_ref, target_ref,
    pair_ref, trans_ref, weight_ref, sig_ref, onehot_ref, row_ref, parts_ref, table_ref,
    edge_ref, xhalo_ref, zhalo_ref, nsend_ref, nrecv_ref,
    part_send, part_recv, halo_send, halo_recv, norm_send, norm_recv, load_sem,
):
    channels, depth, rx, ry = grid_ref.shape
    rays = pix_ref.shape[1]
    chunks = rays // chunk
    total_depth = depth * ns
    span = STEP_SPAN / total_depth
    rows = depth * rx
    slab = lax.axis_index("slab")
    tile = lax.axis_index("tile")

    def slab_peer(d):
        return {"slab": lax.rem(slab + d, ns)}

    def tile_peer(d):
        return {"tile": lax.rem(tile + d, nt)}

    if direct(ns, nt):
        pair = {"tile": tile + 1 - 2 * lax.rem(tile, 2)}
        half = nt // 2
        others = [
            {"slab": lax.rem(slab + k // half, ns), "tile": lax.rem(tile + 2 * (k % half), nt)}
            for k in range(1, ns * half)
        ]
        phases = [[pair], others]
        greeted = [pair] + [{"slab": lax.rem(slab + k // nt, ns), "tile": lax.rem(tile + k % nt, nt)} for k in range(1, ns * nt)]
        greeted = greeted[1:]
    else:
        phases = [[tile_peer(d) for d in range(1, nt)], [slab_peer(d) for d in range(1, ns)]]
        greeted = phases[0] + phases[1]

    loads = [
        pltpu.make_async_copy(grid_hbm.at[c], grid_ref.at[c], load_sem.at[c])
        for c in range(channels)
    ]
    rest = (
        (pix_hbm, pix_ref), (start_hbm, start_ref), (count_hbm, count_ref),
        (target_hbm, target_ref), (first_hbm, first_ref), (second_hbm, second_ref),
    )
    loads += [
        pltpu.make_async_copy(a, b, load_sem.at[channels + i]) for i, (a, b) in enumerate(rest)
    ]
    for copy in loads:
        copy.start()

    barrier = pltpu.get_barrier_semaphore()
    for peer in greeted:
        pl.semaphore_signal(barrier, inc=1, device_id=peer, device_id_type=MESH)

    for c in range(channels):
        loads[c].wait()
    edge_ref[0] = grid_ref[:, :, rx - 1, :]
    edge_ref[1] = grid_ref[:, :, 0, :]

    total = jnp.zeros((rx, ry), jnp.float32)
    before = jnp.ones((rx, ry), jnp.float32)
    sums = [jnp.zeros((rx, ry), jnp.float32) for _ in range(3)]
    for z in range(depth):
        s = grid_ref[0, z]
        e = jnp.exp(-jnp.abs(s))
        tau = (jnp.maximum(s, 0.0) + jnp.log1p(e)) * span
        sig_ref[0, z] = jnp.where(s >= 0, 1.0, e) / (1.0 + e)
        total = total + tau
        after = jnp.exp(-total)
        w = before * (1.0 - jnp.exp(-tau))
        before = after
        trans_ref[z] = after
        weight_ref[z] = w
        for c in range(3):
            col = 1.0 / (1.0 + jnp.exp(-grid_ref[c + 1, z]))
            sig_ref[c + 1, z] = col
            sums[c] = sums[c] + w * col
            table_ref[pl.ds(c * rows + z * rx, rx), :] = sums[c]
        table_ref[pl.ds(3 * rows + z * rx, rx), :] = after
    full = table_ref[...]
    high = full.astype(jnp.bfloat16)
    pair_ref[:, :ry] = high
    pair_ref[:, ry:] = (full - high.astype(jnp.float32)).astype(jnp.bfloat16)

    pl.semaphore_wait(barrier, len(greeted))

    def halo_copy(src, dst, i, peer):
        return pltpu.make_async_remote_copy(
            src_ref=src, dst_ref=dst, send_sem=halo_send.at[i], recv_sem=halo_recv.at[i],
            device_id=peer, device_id_type=MESH)

    halos = [
        (halo_copy(grid_ref.at[:, depth - 1], zhalo_ref.at[0], 0, slab_peer(1)), slab < ns - 1, slab > 0),
        (halo_copy(grid_ref.at[:, 0], zhalo_ref.at[1], 1, slab_peer(ns - 1)), slab > 0, slab < ns - 1),
        (halo_copy(edge_ref.at[0], xhalo_ref.at[0], 2, tile_peer(1)), tile < nt - 1, tile > 0),
        (halo_copy(edge_ref.at[1], xhalo_ref.at[1], 3, tile_peer(nt - 1)), tile > 0, tile < nt - 1),
    ]
    for copy, sends, _ in halos:
        pl.when(sends)(copy.start)

    def part_copy(d, j):
        return pltpu.make_async_remote_copy(
            src_ref=parts_ref.at[slab, j], dst_ref=parts_ref.at[slab, j],
            send_sem=part_send.at[d - 1, j], recv_sem=part_recv.at[d - 1, j],
            device_id=slab_peer(d), device_id_type=MESH)

    def part_wait(d, j):
        source = lax.rem(slab + ns - d, ns)
        pltpu.make_async_remote_copy(
            src_ref=parts_ref.at[source, j], dst_ref=parts_ref.at[source, j],
            send_sem=part_send.at[d - 1, j], recv_sem=part_recv.at[d - 1, j],
            device_id=slab_peer(d), device_id_type=MESH).wait_recv()

    y_ids = lax.broadcasted_iota(jnp.int32, (ry, chunk), 0).astype(jnp.float32).astype(jnp.bfloat16)
    row_ids = lax.broadcasted_iota(jnp.int32, (rows, chunk), 0)

    for copy in loads[channels:channels + 3]:
        copy.wait()
    for j in range(chunks):
        at = pl.ds(j * chunk, chunk)
        pix = pix_ref[:, at]
        start = start_ref[:, at]
        px = pix // ry
        py = (pix - px * ry).astype(jnp.float32).astype(jnp.bfloat16)
        length = jnp.clip((start - slab) * depth + count_ref[:, at], 0, depth)
        length = jnp.where(slab >= start, length, 0)
        row = jnp.where(length > 0, (length - 1) * rx + px, -1)
        row_ref[:, at] = row
        hot = jnp.where(y_ids == py, jnp.ones((), jnp.bfloat16), jnp.zeros((), jnp.bfloat16))
        onehot_ref[:, at] = hot
        twice = jnp.concatenate([hot, hot], axis=0)
        mask = row_ids == row
        for c in range(4):
            block = pl.ds(c * rows, rows)
            u = jnp.dot(pair_ref[block, :], twice, preferred_element_type=jnp.float32)
            part = jnp.sum(jnp.where(mask, u, 0.0), axis=0, keepdims=True)
            if c == 3:
                part = jnp.where(row < 0, 1.0, part)
            parts_ref[slab, j, pl.ds(c, 1), :] = part
        for d in range(1, ns):
            part_copy(d, j).start()

    for copy, _, receives in halos:
        pl.when(receives)(copy.wait_recv)
    x_ids = lax.broadcasted_iota(jnp.int32, (rx, ry), 0)
    lane_ids = lax.broadcasted_iota(jnp.int32, (rx, ry), 1)
    first_x = tile == 0
    last_x = tile == nt - 1
    for c in range(channels):
        for z in range(depth):
            g = grid_ref[c, z]
            if z > 0:
                below = grid_ref[c, z - 1]
            else:
                below = jnp.where(slab > 0, zhalo_ref[0, c], g)
            if z < depth - 1:
                above = grid_ref[c, z + 1]
            else:
                above = jnp.where(slab < ns - 1, zhalo_ref[1, c], g)
            xl = jnp.broadcast_to(xhalo_ref[0, c, pl.ds(z, 1), :], (rx, ry))
            xh = jnp.broadcast_to(xhalo_ref[1, c, pl.ds(z, 1), :], (rx, ry))
            xl = jnp.where(first_x, g, xl)
            xh = jnp.where(last_x, g, xh)
            left = jnp.where(x_ids == 0, xl, pltpu.roll(g, 1, 0))
            right = jnp.where(x_ids == rx - 1, xh, pltpu.roll(g, rx - 1, 0))
            down = jnp.where(lane_ids == 0, g, pltpu.roll(g, 1, 1))
            up = jnp.where(lane_ids == ry - 1, g, pltpu.roll(g, ry - 1, 1))
            smooth = (g - below) + (g - above) + (g - left) + (g - right) + (g - down) + (g - up)
            grad_ref[c, z] = (2.0 * TV_WEIGHT) * smooth

    loads[channels + 3].wait()
    row_ids16 = row_ids.astype(jnp.float32).astype(jnp.bfloat16)
    for j in range(chunks):
        for d in range(1, ns):
            part_wait(d, j)
        at = pl.ds(j * chunk, chunk)
        front_c = jnp.zeros((3, chunk), jnp.float32)
        front_t = jnp.ones((1, chunk), jnp.float32)
        beyond = jnp.full((3, chunk), BACKGROUND, jnp.float32)
        for s in range(ns - 1):
            here = slab > s
            pc = parts_ref[s, j, pl.ds(0, 3), :]
            pt = parts_ref[s, j, pl.ds(3, 1), :]
            front_c = jnp.where(here, front_c + front_t * pc, front_c)
            front_t = jnp.where(here, front_t * pt, front_t)
        for s in range(ns - 1, 0, -1):
            here = slab < s
            pc = parts_ref[s, j, pl.ds(0, 3), :]
            pt = parts_ref[s, j, pl.ds(3, 1), :]
            beyond = jnp.where(here, pc + pt * beyond, beyond)
        pc = parts_ref[slab, j, pl.ds(0, 3), :]
        pt = parts_ref[slab, j, pl.ds(3, 1), :]
        rendered = front_c + front_t * (pc + pt * beyond)
        residual = RENDER_WEIGHT * (rendered - target_ref[:, at])
        color_cot = front_t * residual
        trans_cot = front_t * jnp.sum(residual * beyond, axis=0, keepdims=True)
        hot = onehot_ref[:, at]
        twice = jnp.concatenate([hot, hot], axis=1)
        mask = row_ids16 == row_ref[:, at].astype(jnp.float32).astype(jnp.bfloat16)
        none = jnp.zeros((), jnp.bfloat16)
        for c in range(4):
            cot = color_cot[c:c + 1] if c < 3 else trans_cot
            top = cot.astype(jnp.bfloat16)
            low = (cot - top.astype(jnp.float32)).astype(jnp.bfloat16)
            spread = jnp.concatenate(
                [jnp.where(mask, top, none), jnp.where(mask, low, none)], axis=1)
            u = lax.dot_general(
                spread, twice, (((1,), (1,)), ((), ())), preferred_element_type=jnp.float32)
            block = pl.ds(c * rows, rows)
            if j == 0:
                table_ref[block, :] = u
            else:
                table_ref[block, :] += u

    zero = jnp.zeros((rx, ry), jnp.float32)
    suffix = [zero, zero, zero]
    later = zero
    squares = zero
    for z in range(depth - 1, -1, -1):
        w = weight_ref[z]
        after = trans_ref[z]
        later = later + after * table_ref[pl.ds(3 * rows + z * rx, rx), :]
        dw = zero
        for c in range(3):
            suffix[c] = suffix[c] + table_ref[pl.ds(c * rows + z * rx, rx), :]
            col = sig_ref[c + 1, z]
            dw = dw + col * suffix[c]
            out = grad_ref[c + 1, z] + w * suffix[c] * (col * (1.0 - col))
            grad_ref[c + 1, z] = out
            squares = squares + out * out
        dtau = after * dw - later
        later = later + w * dw
        out = grad_ref[0, z] + dtau * (sig_ref[0, z] * span)
        grad_ref[0, z] = out
        squares = squares + out * out

    local = jnp.sum(squares)

    def norm_copy(phase, slot, peer):
        return pltpu.make_async_remote_copy(
            src_ref=nsend_ref.at[phase], dst_ref=nrecv_ref.at[slot],
            send_sem=norm_send.at[slot], recv_sem=norm_recv.at[slot],
            device_id=peer, device_id_type=MESH)

    value = jnp.full((1, 128), local, jnp.float32)
    copies = []
    base = 0
    for phase, peers in enumerate(phases):
        nsend_ref[phase] = value
        group = [norm_copy(phase, base + i, peer) for i, peer in enumerate(peers)]
        for copy in group:
            copy.start()
        for i, copy in enumerate(group):
            copy.wait_recv()
            value = value + nrecv_ref[base + i]
        base += len(group)
        copies += group
    limit = CLIP_RMS * math.sqrt(4.0 * total_depth * (rx * nt) * ry)
    scale_ref[...] = limit / jnp.maximum(jnp.sqrt(value), limit)
    for copy in loads[channels + 4:]:
        copy.wait()
    for copy in copies:
        copy.wait_send()
    for copy, sends, _ in halos:
        pl.when(sends)(copy.wait_send)
    for j in range(chunks):
        for d in range(1, ns):
            part_copy(d, j).wait_send()


def direct(ns, nt):
    return ns * nt <= DIRECT_LIMIT and nt % 2 == 0


def adam_kernel(
    grid_ref, first_ref, second_ref, grad_ref, scale_ref,
    grid_hbm, first_hbm, second_hbm, grid_out, first_out, second_out, sem,
):
    channels, depth, rx, ry = grid_ref.shape
    scale = jnp.broadcast_to(scale_ref[0:1, 0:1], (rx, ry))
    copies = []
    for c in range(channels):
        for z in range(depth):
            clipped = grad_ref[c, z] * scale
            first = BETA_ONE * first_ref[c, z] + (1.0 - BETA_ONE) * clipped
            second = BETA_TWO * second_ref[c, z] + (1.0 - BETA_TWO) * clipped * clipped
            first_out[c, z] = first
            second_out[c, z] = second
            first_hat = first * (1.0 / (1.0 - BETA_ONE**STEP))
            second_hat = second * (1.0 / (1.0 - BETA_TWO**STEP))
            grid_out[c, z] = grid_ref[c, z] - LEARN_RATE * first_hat / (
                jnp.sqrt(second_hat) + EPSILON)
        pairs = ((first_out, first_hbm), (second_out, second_hbm), (grid_out, grid_hbm))
        for i, (a, b) in enumerate(pairs):
            copy = pltpu.make_async_copy(a.at[c], b.at[c], sem.at[i, c])
            copy.start()
            copies.append(copy)
    for copy in copies:
        copy.wait()


def per_device(voxel_grid, first_moment, second_moment, pixel_index, start_slab, ray_count, target):
    ns = lax.axis_size("slab")
    nt = lax.axis_size("tile")
    channels, depth, rx, ry = voxel_grid.shape
    rays = pixel_index.shape[0]
    chunk = math.gcd(rays, CHUNK)
    chunks = rays // chunk
    rows = depth * rx
    messages = ns * nt // 2 if direct(ns, nt) else nt + ns - 2
    f32 = jnp.float32
    vmem = pl.BlockSpec(memory_space=pltpu.VMEM)
    hbm = pl.BlockSpec(memory_space=pltpu.HBM)
    cells = jax.ShapeDtypeStruct(voxel_grid.shape, f32)
    staged = pl.pallas_call(
        functools.partial(kernel, ns, nt, chunk),
        out_shape=(cells, cells, cells, cells, jax.ShapeDtypeStruct((1, 128), f32)),
        in_specs=[hbm] * 7,
        out_specs=(vmem,) * 5,
        scratch_shapes=[
            pltpu.VMEM((1, rays), jnp.int32),
            pltpu.VMEM((1, rays), jnp.int32),
            pltpu.VMEM((1, rays), jnp.int32),
            pltpu.VMEM(target.shape, f32),
            pltpu.VMEM((channels * rows, 2 * ry), jnp.bfloat16),
            pltpu.VMEM((depth, rx, ry), f32),
            pltpu.VMEM((depth, rx, ry), f32),
            pltpu.VMEM((channels, depth, rx, ry), f32),
            pltpu.VMEM((ry, rays), jnp.bfloat16),
            pltpu.VMEM((1, rays), jnp.int32),
            pltpu.VMEM((ns, chunks, 4, chunk), f32),
            pltpu.VMEM((channels * rows, ry), f32),
            pltpu.VMEM((2, channels, depth, ry), f32),
            pltpu.VMEM((2, channels, depth, ry), f32),
            pltpu.VMEM((2, channels, rx, ry), f32),
            pltpu.VMEM((2, 1, 128), f32),
            pltpu.VMEM((messages, 1, 128), f32),
            pltpu.SemaphoreType.DMA((ns - 1, chunks)),
            pltpu.SemaphoreType.DMA((ns - 1, chunks)),
            pltpu.SemaphoreType.DMA((4,)),
            pltpu.SemaphoreType.DMA((4,)),
            pltpu.SemaphoreType.DMA((messages,)),
            pltpu.SemaphoreType.DMA((messages,)),
            pltpu.SemaphoreType.DMA((channels + 6,)),
        ],
        compiler_params=pltpu.CompilerParams(
            collective_id=0, has_side_effects=True, vmem_limit_bytes=32 * 1024 * 1024
        ),
        name="render_step",
    )(*(pltpu.with_memory_space_constraint(a, pltpu.HBM) for a in (
        voxel_grid,
        first_moment,
        second_moment,
        pixel_index.reshape(1, rays),
        start_slab.reshape(1, rays),
        ray_count.reshape(1, rays),
        target,
    )))
    return pl.pallas_call(
        adam_kernel,
        out_shape=(cells, cells, cells),
        in_specs=[vmem] * 5,
        out_specs=(hbm, hbm, hbm),
        scratch_shapes=[
            pltpu.VMEM(voxel_grid.shape, f32),
            pltpu.VMEM(voxel_grid.shape, f32),
            pltpu.VMEM(voxel_grid.shape, f32),
            pltpu.SemaphoreType.DMA((3, channels)),
        ],
        compiler_params=pltpu.CompilerParams(vmem_limit_bytes=32 * 1024 * 1024),
        name="adam",
    )(*staged)


def solution(mesh):
    cells = P(None, "slab", "tile", None)
    return jax.shard_map(
        per_device,
        mesh=mesh,
        in_specs=(cells, cells, cells, P("tile"), P("tile"), P("tile"), P(None, "tile")),
        out_specs=(cells, cells, cells),
        check_vma=False,
    )
```

profile of v0, /device:TPU:0, one launch (start us, length us, event | category | flops | bytes accessed | tf_op | source)
XLA Modules:
  0.0 24.1 jit_solution(6045972008893178670)
XLA Ops:
  0.6 22.1 %render_step.1 = (f32[4,16,8,256]{3,2,1,0:T(8,128)S(1)}, f32[4,16,8,256]{3,2,1,0:T(8,128)S(1)}, f32[4,16,8,256]{3,2,1,0:T(8,128)S(1)}, f32[4,16,8,256]{3,2,1,0:T(8,128)S(1)}, f32[1,128]{1,0:T(1,128)S(1)}) custom-call(f32[4,16,8,256]{3,2,1,0:T(8,128)} %grid_hbm.1, f32[4,16,8,256]{3,2,1,0:T(8,128)} %first_hbm.1, f32[4,16,8,256]{3,2,1,0:T(8,128)} %second_hbm.1, ...), custom_call_target="tpu_custom_call" | custom-call | tf_op jit(solution)/shard_map/render_step/pallas_call | solution.py:342
  22.7 1.4 %adam.1 = (f32[4,16,8,256]{3,2,1,0:T(8,128)}, f32[4,16,8,256]{3,2,1,0:T(8,128)}, f32[4,16,8,256]{3,2,1,0:T(8,128)}) custom-call(f32[4,16,8,256]{3,2,1,0:T(8,128)S(1)} %get-tuple-element.8.grid_ref, f32[4,16,8,256]{3,2,1,0:T(8,128)S(1)} %get-tuple-element.9.first_ref, f32[4,16,8,256]{3,2,1,0:T(8,128)S(1)} %get-tuple-element.10.second_ref, ...), custom_call_target="tpu_custom_call" | custom-call | tf_op jit(solution)/shard_map/adam/pallas_call | solution.py:386
where the time goes:
time: 24.2 us; the launch traced here: 24.1 us
  Pallas kernels  23.5 us (97%)
  between operations  0.64 us (3%)
    pallas_call x1, Pallas kernels, per_device(): pl.pallas_call(functools.partial(kernel, ns, nt, chunk), out_shape=(cells...  22.1 us
    pallas_call x1, Pallas kernels, per_device(): pl.pallas_call(adam_kernel, out_shape=(cells, cells, cells), in_specs=[vm...  1.39 us

commit v1 on v0

--- a/solution.py
+++ b/solution.py
@@ -30,12 +30,13 @@
     pix_ref, start_ref, count_ref, target_ref,
     pair_ref, trans_ref, weight_ref, sig_ref, onehot_ref, row_ref, parts_ref, table_ref,
     edge_ref, xhalo_ref, zhalo_ref, nsend_ref, nrecv_ref,
-    part_send, part_recv, halo_send, halo_recv, norm_send, norm_recv, load_sem,
+    part_send, part_recv, ready_sem, halo_send, halo_recv, norm_send, norm_recv, load_sem,
 ):
     channels, depth, rx, ry = grid_ref.shape
     rays = pix_ref.shape[1]
     chunks = rays // chunk
     total_depth = depth * ns
+    reach = span_reach(ns)
     span = STEP_SPAN / total_depth
     rows = depth * rx
     slab = lax.axis_index("slab")
@@ -55,11 +56,15 @@
             for k in range(1, ns * half)
         ]
         phases = [[pair], others]
-        greeted = [pair] + [{"slab": lax.rem(slab + k // nt, ns), "tile": lax.rem(tile + k % nt, nt)} for k in range(1, ns * nt)]
-        greeted = greeted[1:]
+        near = reach
     else:
         phases = [[tile_peer(d) for d in range(1, nt)], [slab_peer(d) for d in range(1, ns)]]
-        greeted = phases[0] + phases[1]
+        near = ns - 1
+    offsets = [k for k in range(-near, near + 1) if k]
+    travels = [k for k in range(-reach, reach + 1) if k]
+
+    def inside(s):
+        return (s >= 0) & (s < ns)
 
     loads = [
         pltpu.make_async_copy(grid_hbm.at[c], grid_ref.at[c], load_sem.at[c])
@@ -76,8 +81,15 @@
         copy.start()
 
     barrier = pltpu.get_barrier_semaphore()
-    for peer in greeted:
-        pl.semaphore_signal(barrier, inc=1, device_id=peer, device_id_type=MESH)
+    for d in range(1, nt):
+        pl.semaphore_signal(barrier, inc=1, device_id=tile_peer(d), device_id_type=MESH)
+    greeters = nt - 1
+    for k in offsets:
+        @pl.when(inside(slab + k))
+        def _(k=k):
+            pl.semaphore_signal(
+                barrier, inc=1, device_id={"slab": slab + k}, device_id_type=MESH)
+        greeters = greeters + inside(slab + k).astype(jnp.int32)
 
     for c in range(channels):
         loads[c].wait()
@@ -109,7 +121,7 @@
     pair_ref[:, :ry] = high
     pair_ref[:, ry:] = (full - high.astype(jnp.float32)).astype(jnp.bfloat16)
 
-    pl.semaphore_wait(barrier, len(greeted))
+    pl.semaphore_wait(barrier, greeters)
 
     def halo_copy(src, dst, i, peer):
         return pltpu.make_async_remote_copy(
@@ -125,18 +137,21 @@
     for copy, sends, _ in halos:
         pl.when(sends)(copy.start)
 
-    def part_copy(d, j):
+    def part_copy(k, j, source):
+        lane = travels.index(k)
         return pltpu.make_async_remote_copy(
-            src_ref=parts_ref.at[slab, j], dst_ref=parts_ref.at[slab, j],
-            send_sem=part_send.at[d - 1, j], recv_sem=part_recv.at[d - 1, j],
-            device_id=slab_peer(d), device_id_type=MESH)
-
-    def part_wait(d, j):
-        source = lax.rem(slab + ns - d, ns)
-        pltpu.make_async_remote_copy(
             src_ref=parts_ref.at[source, j], dst_ref=parts_ref.at[source, j],
-            send_sem=part_send.at[d - 1, j], recv_sem=part_recv.at[d - 1, j],
-            device_id=slab_peer(d), device_id_type=MESH).wait_recv()
+            send_sem=part_send.at[lane, j], recv_sem=part_recv.at[lane, j],
+            device_id={"slab": source + k}, device_id_type=MESH)
+
+    def part_start(k, j):
+        pl.when(inside(slab + k))(lambda: part_copy(k, j, slab).start())
+
+    def part_sent(k, j):
+        pl.when(inside(slab + k))(lambda: part_copy(k, j, slab).wait_send())
+
+    def part_wait(k, j):
+        pl.when(inside(slab - k))(lambda: part_copy(k, j, slab - k).wait_recv())
 
     y_ids = lax.broadcasted_iota(jnp.int32, (ry, chunk), 0).astype(jnp.float32).astype(jnp.bfloat16)
     row_ids = lax.broadcasted_iota(jnp.int32, (rows, chunk), 0)
@@ -155,17 +170,17 @@
         row_ref[:, at] = row
         hot = jnp.where(y_ids == py, jnp.ones((), jnp.bfloat16), jnp.zeros((), jnp.bfloat16))
         onehot_ref[:, at] = hot
-        twice = jnp.concatenate([hot, hot], axis=0)
         mask = row_ids == row
+        u = jnp.dot(pair_ref[:, :ry], hot, preferred_element_type=jnp.float32)
+        u = u + jnp.dot(pair_ref[:, ry:], hot, preferred_element_type=jnp.float32)
         for c in range(4):
-            block = pl.ds(c * rows, rows)
-            u = jnp.dot(pair_ref[block, :], twice, preferred_element_type=jnp.float32)
-            part = jnp.sum(jnp.where(mask, u, 0.0), axis=0, keepdims=True)
+            picked = jnp.where(mask, u[c * rows:(c + 1) * rows], 0.0)
+            part = jnp.sum(picked, axis=0, keepdims=True)
             if c == 3:
                 part = jnp.where(row < 0, 1.0, part)
             parts_ref[slab, j, pl.ds(c, 1), :] = part
-        for d in range(1, ns):
-            part_copy(d, j).start()
+        for k in travels:
+            part_start(k, j)
 
     for copy, _, receives in halos:
         pl.when(receives)(copy.wait_recv)
@@ -198,22 +213,30 @@
     loads[channels + 3].wait()
     row_ids16 = row_ids.astype(jnp.float32).astype(jnp.bfloat16)
     for j in range(chunks):
-        for d in range(1, ns):
-            part_wait(d, j)
+        for k in travels:
+            part_wait(k, j)
+        if j == 0 and direct(ns, nt):
+            for k in (-reach, reach):
+                @pl.when(inside(slab + k))
+                def _(k=k):
+                    pl.semaphore_signal(
+                        ready_sem, inc=1, device_id={"slab": slab + k}, device_id_type=MESH)
         at = pl.ds(j * chunk, chunk)
         front_c = jnp.zeros((3, chunk), jnp.float32)
         front_t = jnp.ones((1, chunk), jnp.float32)
         beyond = jnp.full((3, chunk), BACKGROUND, jnp.float32)
-        for s in range(ns - 1):
-            here = slab > s
-            pc = parts_ref[s, j, pl.ds(0, 3), :]
-            pt = parts_ref[s, j, pl.ds(3, 1), :]
+        for k in range(reach, 0, -1):
+            here = slab >= k
+            source = jnp.maximum(slab - k, 0)
+            pc = parts_ref[source, j, pl.ds(0, 3), :]
+            pt = parts_ref[source, j, pl.ds(3, 1), :]
             front_c = jnp.where(here, front_c + front_t * pc, front_c)
             front_t = jnp.where(here, front_t * pt, front_t)
-        for s in range(ns - 1, 0, -1):
-            here = slab < s
-            pc = parts_ref[s, j, pl.ds(0, 3), :]
-            pt = parts_ref[s, j, pl.ds(3, 1), :]
+        for k in range(reach, 0, -1):
+            here = slab + k < ns
+            source = jnp.minimum(slab + k, ns - 1)
+            pc = parts_ref[source, j, pl.ds(0, 3), :]
+            pt = parts_ref[source, j, pl.ds(3, 1), :]
             beyond = jnp.where(here, pc + pt * beyond, beyond)
         pc = parts_ref[slab, j, pl.ds(0, 3), :]
         pt = parts_ref[slab, j, pl.ds(3, 1), :]
@@ -222,22 +245,25 @@
         color_cot = front_t * residual
         trans_cot = front_t * jnp.sum(residual * beyond, axis=0, keepdims=True)
         hot = onehot_ref[:, at]
-        twice = jnp.concatenate([hot, hot], axis=1)
         mask = row_ids16 == row_ref[:, at].astype(jnp.float32).astype(jnp.bfloat16)
         none = jnp.zeros((), jnp.bfloat16)
+        tops = []
+        lows = []
         for c in range(4):
             cot = color_cot[c:c + 1] if c < 3 else trans_cot
             top = cot.astype(jnp.bfloat16)
             low = (cot - top.astype(jnp.float32)).astype(jnp.bfloat16)
-            spread = jnp.concatenate(
-                [jnp.where(mask, top, none), jnp.where(mask, low, none)], axis=1)
-            u = lax.dot_general(
-                spread, twice, (((1,), (1,)), ((), ())), preferred_element_type=jnp.float32)
-            block = pl.ds(c * rows, rows)
-            if j == 0:
-                table_ref[block, :] = u
-            else:
-                table_ref[block, :] += u
+            tops.append(jnp.where(mask, top, none))
+            lows.append(jnp.where(mask, low, none))
+        u = sum(
+            lax.dot_general(
+                jnp.concatenate(spread, axis=0), hot, (((1,), (1,)), ((), ())),
+                preferred_element_type=jnp.float32)
+            for spread in (tops, lows))
+        if j == 0:
+            table_ref[...] = u
+        else:
+            table_ref[...] += u
 
     zero = jnp.zeros((rx, ry), jnp.float32)
     suffix = [zero, zero, zero]
@@ -269,6 +295,9 @@
             send_sem=norm_send.at[slot], recv_sem=norm_recv.at[slot],
             device_id=peer, device_id_type=MESH)
 
+    if direct(ns, nt):
+        far = inside(slab - reach).astype(jnp.int32) + inside(slab + reach).astype(jnp.int32)
+        pl.semaphore_wait(ready_sem, far)
     value = jnp.full((1, 128), local, jnp.float32)
     copies = []
     base = 0
@@ -291,8 +320,12 @@
     for copy, sends, _ in halos:
         pl.when(sends)(copy.wait_send)
     for j in range(chunks):
-        for d in range(1, ns):
-            part_copy(d, j).wait_send()
+        for k in travels:
+            part_sent(k, j)
+
+
+def span_reach(ns):
+    return max(ns // 2, 1)
 
 
 def direct(ns, nt):
@@ -362,8 +395,9 @@
             pltpu.VMEM((2, channels, rx, ry), f32),
             pltpu.VMEM((2, 1, 128), f32),
             pltpu.VMEM((messages, 1, 128), f32),
-            pltpu.SemaphoreType.DMA((ns - 1, chunks)),
-            pltpu.SemaphoreType.DMA((ns - 1, chunks)),
+            pltpu.SemaphoreType.DMA((2 * span_reach(ns), chunks)),
+            pltpu.SemaphoreType.DMA((2 * span_reach(ns), chunks)),
+            pltpu.SemaphoreType.REGULAR,
             pltpu.SemaphoreType.DMA((4,)),
             pltpu.SemaphoreType.DMA((4,)),
             pltpu.SemaphoreType.DMA((messages,)),

time: 24.2 us -> 25 us (1.033)
  Pallas kernels: 23.5 us -> 24.2 us
    pallas_call x1, Pallas kernels: 22.1 us -> 22.8 us  [per_device(): pl.pallas_call(functools.partial(kernel, ns, nt, chunk), out_shape=(cells...]
where the time goes in v1:
time: 25 us; the launch traced here: 24.8 us
  Pallas kernels  24.2 us (97%)
  between operations  0.64 us (3%)
    pallas_call x1, Pallas kernels, per_device(): pl.pallas_call(functools.partial(kernel, ns, nt, chunk), out_shape=(cells...  22.8 us
    pallas_call x1, Pallas kernels, per_device(): pl.pallas_call(adam_kernel, out_shape=(cells, cells, cells), in_specs=[vm...  1.39 us

profile of v1, /device:TPU:0, one launch (start us, length us, event | category | flops | bytes accessed | tf_op | source)
XLA Modules:
  0.0 24.8 jit_solution(3091173822882215999)
XLA Ops:
  0.6 22.8 %render_step.1 = (f32[4,16,8,256]{3,2,1,0:T(8,128)S(1)}, f32[4,16,8,256]{3,2,1,0:T(8,128)S(1)}, f32[4,16,8,256]{3,2,1,0:T(8,128)S(1)}, f32[4,16,8,256]{3,2,1,0:T(8,128)S(1)}, f32[1,128]{1,0:T(1,128)S(1)}) custom-call(f32[4,16,8,256]{3,2,1,0:T(8,128)} %grid_hbm.1, f32[4,16,8,256]{3,2,1,0:T(8,128)} %first_hbm.1, f32[4,16,8,256]{3,2,1,0:T(8,128)} %second_hbm.1, ...), custom_call_target="tpu_custom_call" | custom-call | tf_op jit(solution)/shard_map/render_step/pallas_call | solution.py:375
  23.4 1.4 %adam.1 = (f32[4,16,8,256]{3,2,1,0:T(8,128)}, f32[4,16,8,256]{3,2,1,0:T(8,128)}, f32[4,16,8,256]{3,2,1,0:T(8,128)}) custom-call(f32[4,16,8,256]{3,2,1,0:T(8,128)S(1)} %get-tuple-element.8.grid_ref, f32[4,16,8,256]{3,2,1,0:T(8,128)S(1)} %get-tuple-element.9.first_ref, f32[4,16,8,256]{3,2,1,0:T(8,128)S(1)} %get-tuple-element.10.second_ref, ...), custom_call_target="tpu_custom_call" | custom-call | tf_op jit(solution)/shard_map/adam/pallas_call | solution.py:420

commit v2 on v1

--- a/solution.py
+++ b/solution.py
@@ -18,7 +18,7 @@
 BETA_ONE = 0.9
 BETA_TWO = 0.99
 EPSILON = 1e-08
-CHUNK = 512
+CHUNK = 1024
 DIRECT_LIMIT = 64
 MESH = pl.DeviceIdType.MESH
 
@@ -28,9 +28,10 @@
     grid_hbm, first_hbm, second_hbm, pix_hbm, start_hbm, count_hbm, target_hbm,
     grid_ref, first_ref, second_ref, grad_ref, scale_ref,
     pix_ref, start_ref, count_ref, target_ref,
-    pair_ref, trans_ref, weight_ref, sig_ref, onehot_ref, row_ref, parts_ref, table_ref,
+    pair_ref, trans_ref, weight_ref, sig_ref, onehot_ref, row_ref, table_ref,
+    whole_ref, wholes_ref, front_ref, own_ref, last_ref, near_ref, far_ref,
     edge_ref, xhalo_ref, zhalo_ref, nsend_ref, nrecv_ref,
-    part_send, part_recv, ready_sem, halo_send, halo_recv, norm_send, norm_recv, load_sem,
+    whole_send, whole_recv, part_send, part_recv, ready_sem, halo_send, halo_recv, norm_send, norm_recv, load_sem,
 ):
     channels, depth, rx, ry = grid_ref.shape
     rays = pix_ref.shape[1]
@@ -61,7 +62,6 @@
         phases = [[tile_peer(d) for d in range(1, nt)], [slab_peer(d) for d in range(1, ns)]]
         near = ns - 1
     offsets = [k for k in range(-near, near + 1) if k]
-    travels = [k for k in range(-reach, reach + 1) if k]
 
     def inside(s):
         return (s >= 0) & (s < ns)
@@ -116,12 +116,24 @@
             sums[c] = sums[c] + w * col
             table_ref[pl.ds(c * rows + z * rx, rx), :] = sums[c]
         table_ref[pl.ds(3 * rows + z * rx, rx), :] = after
+    for c in range(3):
+        whole_ref[c] = sums[c]
+    whole_ref[3] = before
     full = table_ref[...]
     high = full.astype(jnp.bfloat16)
     pair_ref[:, :ry] = high
     pair_ref[:, ry:] = (full - high.astype(jnp.float32)).astype(jnp.bfloat16)
 
     pl.semaphore_wait(barrier, greeters)
+
+    def whole_copy(k):
+        return pltpu.make_async_remote_copy(
+            src_ref=whole_ref, dst_ref=wholes_ref.at[k - 1],
+            send_sem=whole_send.at[k - 1], recv_sem=whole_recv.at[k - 1],
+            device_id=slab_peer(k), device_id_type=MESH)
+
+    for k in range(reach, 0, -1):
+        pl.when(slab + k < ns)(whole_copy(k).start)
 
     def halo_copy(src, dst, i, peer):
         return pltpu.make_async_remote_copy(
@@ -137,21 +149,12 @@
     for copy, sends, _ in halos:
         pl.when(sends)(copy.start)
 
-    def part_copy(k, j, source):
-        lane = travels.index(k)
+    def part_copy(k, j):
+        src, dst = (last_ref, far_ref) if k == reach else (own_ref, near_ref.at[k - 1])
         return pltpu.make_async_remote_copy(
-            src_ref=parts_ref.at[source, j], dst_ref=parts_ref.at[source, j],
-            send_sem=part_send.at[lane, j], recv_sem=part_recv.at[lane, j],
-            device_id={"slab": source + k}, device_id_type=MESH)
-
-    def part_start(k, j):
-        pl.when(inside(slab + k))(lambda: part_copy(k, j, slab).start())
-
-    def part_sent(k, j):
-        pl.when(inside(slab + k))(lambda: part_copy(k, j, slab).wait_send())
-
-    def part_wait(k, j):
-        pl.when(inside(slab - k))(lambda: part_copy(k, j, slab - k).wait_recv())
+            src_ref=src.at[j], dst_ref=dst.at[j],
+            send_sem=part_send.at[k - 1, j], recv_sem=part_recv.at[k - 1, j],
+            device_id=slab_peer(ns - k), device_id_type=MESH)
 
     y_ids = lax.broadcasted_iota(jnp.int32, (ry, chunk), 0).astype(jnp.float32).astype(jnp.bfloat16)
     row_ids = lax.broadcasted_iota(jnp.int32, (rows, chunk), 0)
@@ -178,9 +181,11 @@
             part = jnp.sum(picked, axis=0, keepdims=True)
             if c == 3:
                 part = jnp.where(row < 0, 1.0, part)
-            parts_ref[slab, j, pl.ds(c, 1), :] = part
-        for k in travels:
-            part_start(k, j)
+            own_ref[j, pl.ds(c, 1), :] = part
+        for c in range(3):
+            last_ref[j, c] = own_ref[j, pl.ds(c, 1), :] + BACKGROUND * part
+        for k in range(1, reach + 1):
+            pl.when(slab >= k)(part_copy(k, j).start)
 
     for copy, _, receives in halos:
         pl.when(receives)(copy.wait_recv)
@@ -210,11 +215,42 @@
             smooth = (g - below) + (g - above) + (g - left) + (g - right) + (g - down) + (g - up)
             grad_ref[c, z] = (2.0 * TV_WEIGHT) * smooth
 
+    for k in range(1, reach + 1):
+        pl.when(slab >= k)(whole_copy(k).wait_recv)
+    folded = [[] for _ in range(4)]
+    fold_t = jnp.ones((rx, ry), jnp.float32)
+    fold_c = [jnp.zeros((rx, ry), jnp.float32)] * 3
+    for k in range(1, reach + 1):
+        there = slab >= k
+        t = wholes_ref[k - 1, 3]
+        fold_c = [jnp.where(there, wholes_ref[k - 1, c] + t * fold_c[c], 0.0) for c in range(3)]
+        fold_t = jnp.where(there, t * fold_t, 0.0)
+        for c in range(4):
+            folded[c].append(fold_c[c] if c < 3 else fold_t)
+    folds = jnp.concatenate([f for fs in folded for f in fs], axis=0)
+    fold_high = folds.astype(jnp.bfloat16)
+    fold_low = (folds - fold_high.astype(jnp.float32)).astype(jnp.bfloat16)
+    step_rows = reach * rx
+    step_ids = lax.broadcasted_iota(jnp.int32, (step_rows, chunk), 0)
+    for j in range(chunks):
+        at = pl.ds(j * chunk, chunk)
+        hot = onehot_ref[:, at]
+        behind = slab - start_ref[:, at]
+        mask = step_ids == (behind - 1) * rx + pix_ref[:, at] // ry
+        u = jnp.dot(fold_high, hot, preferred_element_type=jnp.float32)
+        u = u + jnp.dot(fold_low, hot, preferred_element_type=jnp.float32)
+        for c in range(4):
+            picked = jnp.where(mask, u[c * step_rows:(c + 1) * step_rows], 0.0)
+            value = jnp.sum(picked, axis=0, keepdims=True)
+            if c == 3:
+                value = jnp.where(behind <= 0, 1.0, value)
+            front_ref[j, pl.ds(c, 1), :] = value
+
     loads[channels + 3].wait()
     row_ids16 = row_ids.astype(jnp.float32).astype(jnp.bfloat16)
     for j in range(chunks):
-        for k in travels:
-            part_wait(k, j)
+        for k in range(1, reach + 1):
+            pl.when(slab + k < ns)(part_copy(k, j).wait_recv)
         if j == 0 and direct(ns, nt):
             for k in (-reach, reach):
                 @pl.when(inside(slab + k))
@@ -222,24 +258,16 @@
                     pl.semaphore_signal(
                         ready_sem, inc=1, device_id={"slab": slab + k}, device_id_type=MESH)
         at = pl.ds(j * chunk, chunk)
-        front_c = jnp.zeros((3, chunk), jnp.float32)
-        front_t = jnp.ones((1, chunk), jnp.float32)
-        beyond = jnp.full((3, chunk), BACKGROUND, jnp.float32)
-        for k in range(reach, 0, -1):
-            here = slab >= k
-            source = jnp.maximum(slab - k, 0)
-            pc = parts_ref[source, j, pl.ds(0, 3), :]
-            pt = parts_ref[source, j, pl.ds(3, 1), :]
-            front_c = jnp.where(here, front_c + front_t * pc, front_c)
-            front_t = jnp.where(here, front_t * pt, front_t)
-        for k in range(reach, 0, -1):
-            here = slab + k < ns
-            source = jnp.minimum(slab + k, ns - 1)
-            pc = parts_ref[source, j, pl.ds(0, 3), :]
-            pt = parts_ref[source, j, pl.ds(3, 1), :]
-            beyond = jnp.where(here, pc + pt * beyond, beyond)
-        pc = parts_ref[slab, j, pl.ds(0, 3), :]
-        pt = parts_ref[slab, j, pl.ds(3, 1), :]
+        front_c = front_ref[j, pl.ds(0, 3), :]
+        front_t = front_ref[j, pl.ds(3, 1), :]
+        beyond = jnp.concatenate([far_ref[j, c] for c in range(3)], axis=0)
+        beyond = jnp.where(slab + reach < ns, beyond, BACKGROUND)
+        for k in range(reach - 1, 0, -1):
+            pc = near_ref[k - 1, j, pl.ds(0, 3), :]
+            pt = near_ref[k - 1, j, pl.ds(3, 1), :]
+            beyond = jnp.where(slab + k < ns, pc + pt * beyond, beyond)
+        pc = own_ref[j, pl.ds(0, 3), :]
+        pt = own_ref[j, pl.ds(3, 1), :]
         rendered = front_c + front_t * (pc + pt * beyond)
         residual = RENDER_WEIGHT * (rendered - target_ref[:, at])
         color_cot = front_t * residual
@@ -320,8 +348,10 @@
     for copy, sends, _ in halos:
         pl.when(sends)(copy.wait_send)
     for j in range(chunks):
-        for k in travels:
-            part_sent(k, j)
+        for k in range(1, reach + 1):
+            pl.when(slab >= k)(part_copy(k, j).wait_send)
+    for k in range(1, reach + 1):
+        pl.when(slab + k < ns)(whole_copy(k).wait_send)
 
 
 def span_reach(ns):
@@ -367,6 +397,7 @@
     chunk = math.gcd(rays, CHUNK)
     chunks = rays // chunk
     rows = depth * rx
+    reach = span_reach(ns)
     messages = ns * nt // 2 if direct(ns, nt) else nt + ns - 2
     f32 = jnp.float32
     vmem = pl.BlockSpec(memory_space=pltpu.VMEM)
@@ -388,15 +419,23 @@
             pltpu.VMEM((channels, depth, rx, ry), f32),
             pltpu.VMEM((ry, rays), jnp.bfloat16),
             pltpu.VMEM((1, rays), jnp.int32),
-            pltpu.VMEM((ns, chunks, 4, chunk), f32),
             pltpu.VMEM((channels * rows, ry), f32),
+            pltpu.VMEM((4, rx, ry), f32),
+            pltpu.VMEM((reach, 4, rx, ry), f32),
+            pltpu.VMEM((chunks, 4, chunk), f32),
+            pltpu.VMEM((chunks, 4, chunk), f32),
+            pltpu.VMEM((chunks, 3, 1, chunk), f32),
+            pltpu.VMEM((max(reach - 1, 1), chunks, 4, chunk), f32),
+            pltpu.VMEM((chunks, 3, 1, chunk), f32),
             pltpu.VMEM((2, channels, depth, ry), f32),
             pltpu.VMEM((2, channels, depth, ry), f32),
             pltpu.VMEM((2, channels, rx, ry), f32),
             pltpu.VMEM((2, 1, 128), f32),
             pltpu.VMEM((messages, 1, 128), f32),
-            pltpu.SemaphoreType.DMA((2 * span_reach(ns), chunks)),
-            pltpu.SemaphoreType.DMA((2 * span_reach(ns), chunks)),
+            pltpu.SemaphoreType.DMA((reach,)),
+            pltpu.SemaphoreType.DMA((reach,)),
+            pltpu.SemaphoreType.DMA((reach, chunks)),
+            pltpu.SemaphoreType.DMA((reach, chunks)),
             pltpu.SemaphoreType.REGULAR,
             pltpu.SemaphoreType.DMA((4,)),
             pltpu.SemaphoreType.DMA((4,)),

time: 25 us -> 24.7 us (0.988)
  Pallas kernels: 24.2 us -> 23.9 us
where the time goes in v2:
time: 24.7 us; the launch traced here: 24.6 us
  Pallas kernels  23.9 us (97%)
  between operations  0.64 us (3%)
    pallas_call x1, Pallas kernels, per_device(): pl.pallas_call(functools.partial(kernel, ns, nt, chunk), out_shape=(cells...  22.5 us
    pallas_call x1, Pallas kernels, per_device(): pl.pallas_call(adam_kernel, out_shape=(cells, cells, cells), in_specs=[vm...  1.39 us

profile of v2, /device:TPU:0, one launch (start us, length us, event | category | flops | bytes accessed | tf_op | source)
XLA Modules:
  0.0 24.6 jit_solution(13290524102242967346)
XLA Ops:
  0.6 22.5 %render_step.1 = (f32[4,16,8,256]{3,2,1,0:T(8,128)S(1)}, f32[4,16,8,256]{3,2,1,0:T(8,128)S(1)}, f32[4,16,8,256]{3,2,1,0:T(8,128)S(1)}, f32[4,16,8,256]{3,2,1,0:T(8,128)S(1)}, f32[1,128]{1,0:T(1,128)S(1)}) custom-call(f32[4,16,8,256]{3,2,1,0:T(8,128)} %grid_hbm.1, f32[4,16,8,256]{3,2,1,0:T(8,128)} %first_hbm.1, f32[4,16,8,256]{3,2,1,0:T(8,128)} %second_hbm.1, ...), custom_call_target="tpu_custom_call" | custom-call | tf_op jit(solution)/shard_map/render_step/pallas_call | solution.py:406
  23.2 1.4 %adam.1 = (f32[4,16,8,256]{3,2,1,0:T(8,128)}, f32[4,16,8,256]{3,2,1,0:T(8,128)}, f32[4,16,8,256]{3,2,1,0:T(8,128)}) custom-call(f32[4,16,8,256]{3,2,1,0:T(8,128)S(1)} %get-tuple-element.8.grid_ref, f32[4,16,8,256]{3,2,1,0:T(8,128)S(1)} %get-tuple-element.9.first_ref, f32[4,16,8,256]{3,2,1,0:T(8,128)S(1)} %get-tuple-element.10.second_ref, ...), custom_call_target="tpu_custom_call" | custom-call | tf_op jit(solution)/shard_map/adam/pallas_call | solution.py:459

commit v3 on v2

--- a/solution.py
+++ b/solution.py
@@ -18,7 +18,8 @@
 BETA_ONE = 0.9
 BETA_TWO = 0.99
 EPSILON = 1e-08
-CHUNK = 1024
+CHUNK = 512
+WIDTH = 256
 DIRECT_LIMIT = 64
 MESH = pl.DeviceIdType.MESH
 
@@ -161,31 +162,51 @@
 
     for copy in loads[channels:channels + 3]:
         copy.wait()
-    for j in range(chunks):
-        at = pl.ds(j * chunk, chunk)
-        pix = pix_ref[:, at]
-        start = start_ref[:, at]
-        px = pix // ry
-        py = (pix - px * ry).astype(jnp.float32).astype(jnp.bfloat16)
-        length = jnp.clip((start - slab) * depth + count_ref[:, at], 0, depth)
-        length = jnp.where(slab >= start, length, 0)
-        row = jnp.where(length > 0, (length - 1) * rx + px, -1)
-        row_ref[:, at] = row
-        hot = jnp.where(y_ids == py, jnp.ones((), jnp.bfloat16), jnp.zeros((), jnp.bfloat16))
-        onehot_ref[:, at] = hot
-        mask = row_ids == row
-        u = jnp.dot(pair_ref[:, :ry], hot, preferred_element_type=jnp.float32)
-        u = u + jnp.dot(pair_ref[:, ry:], hot, preferred_element_type=jnp.float32)
-        for c in range(4):
-            picked = jnp.where(mask, u[c * rows:(c + 1) * rows], 0.0)
-            part = jnp.sum(picked, axis=0, keepdims=True)
-            if c == 3:
-                part = jnp.where(row < 0, 1.0, part)
-            own_ref[j, pl.ds(c, 1), :] = part
-        for c in range(3):
-            last_ref[j, c] = own_ref[j, pl.ds(c, 1), :] + BACKGROUND * part
-        for k in range(1, reach + 1):
-            pl.when(slab >= k)(part_copy(k, j).start)
+    units = range(chunk // WIDTH)
+
+    def gather(*accs):
+        banks = [[accs[(b * len(units) + q) * 4:][:4] for q in units] for b in range(2)]
+        for j in range(chunks + 1):
+            if j < chunks:
+                at = pl.ds(j * chunk, chunk)
+                pix = pix_ref[:, at]
+                start = start_ref[:, at]
+                px = pix // ry
+                py = (pix - px * ry).astype(jnp.float32).astype(jnp.bfloat16)
+                length = jnp.clip((start - slab) * depth + count_ref[:, at], 0, depth)
+                length = jnp.where(slab >= start, length, 0)
+                row_ref[:, at] = jnp.where(length > 0, (length - 1) * rx + px, -1)
+                hot = jnp.where(y_ids == py, jnp.ones((), jnp.bfloat16), jnp.zeros((), jnp.bfloat16))
+                onehot_ref[:, at] = hot
+                for q in units:
+                    pltpu.matmul_push_rhs(hot[:, q * WIDTH:(q + 1) * WIDTH], j % 2, q)
+                for c in range(4):
+                    block = pl.ds(c * rows, rows)
+                    for half in range(2):
+                        lhs = pair_ref[block, half * ry:(half + 1) * ry]
+                        for q in units:
+                            fresh = j % 2 if c == 0 and half == 0 else None
+                            pltpu.matmul_acc_lhs(banks[j % 2][q][c], lhs, fresh)
+            if j == 0:
+                continue
+            i = j - 1
+            row = row_ref[:, pl.ds(i * chunk, chunk)]
+            mask = row_ids == row
+            for c in range(4):
+                u = jnp.concatenate([pltpu.matmul_pop(banks[i % 2][q][c]) for q in units], axis=1)
+                part = jnp.sum(jnp.where(mask, u, 0.0), axis=0, keepdims=True)
+                if c == 3:
+                    part = jnp.where(row < 0, 1.0, part)
+                own_ref[i, pl.ds(c, 1), :] = part
+            for c in range(3):
+                last_ref[i, c] = own_ref[i, pl.ds(c, 1), :] + BACKGROUND * part
+            for k in range(1, reach + 1):
+                pl.when(slab >= k)(part_copy(k, i).start)
+
+    pl.run_scoped(gather, *[
+        pltpu.ACC(q)((rows, WIDTH), jnp.float32)
+        for _ in range(2) for q in units for _ in range(4)
+    ])
 
     for copy, _, receives in halos:
         pl.when(receives)(copy.wait_recv)
@@ -232,66 +253,84 @@
     fold_low = (folds - fold_high.astype(jnp.float32)).astype(jnp.bfloat16)
     step_rows = reach * rx
     step_ids = lax.broadcasted_iota(jnp.int32, (step_rows, chunk), 0)
-    for j in range(chunks):
-        at = pl.ds(j * chunk, chunk)
-        hot = onehot_ref[:, at]
-        behind = slab - start_ref[:, at]
-        mask = step_ids == (behind - 1) * rx + pix_ref[:, at] // ry
-        u = jnp.dot(fold_high, hot, preferred_element_type=jnp.float32)
-        u = u + jnp.dot(fold_low, hot, preferred_element_type=jnp.float32)
+    row_ids16 = row_ids.astype(jnp.float32).astype(jnp.bfloat16)
+    none = jnp.zeros((), jnp.bfloat16)
+    lags = 4
+
+    def scatter(*accs):
+        sums_acc = [accs[q * 4:][:4] for q in units]
+        accs = accs[4 * len(units):]
+        steps = [[accs[b * len(units) + q] for q in units] for b in range(lags)]
+
+        def columns(j, q):
+            return onehot_ref[:, pl.ds(j * chunk + q * WIDTH, WIDTH)]
+
+        for j in range(chunks):
+            at = pl.ds(j * chunk, chunk)
+            for q in units:
+                pltpu.matmul_push_rhs(columns(j, q), j % 2, q)
+            for half, lhs in enumerate((fold_high, fold_low)):
+                for q in units:
+                    pltpu.matmul_acc_lhs(steps[j % lags][q], lhs, None if half else j % 2)
+            behind = slab - start_ref[:, at]
+            mask = step_ids == (behind - 1) * rx + pix_ref[:, at] // ry
+            u = jnp.concatenate([pltpu.matmul_pop(steps[j % lags][q]) for q in units], axis=1)
+            for c in range(4):
+                picked = jnp.where(mask, u[c * step_rows:(c + 1) * step_rows], 0.0)
+                value = jnp.sum(picked, axis=0, keepdims=True)
+                if c == 3:
+                    value = jnp.where(behind <= 0, 1.0, value)
+                front_ref[j, pl.ds(c, 1), :] = value
+
+        loads[channels + 3].wait()
+        for q in units:
+            pltpu.matmul_push_rhs(columns(0, q), 0, q, transpose=True)
+        for j in range(chunks):
+            for k in range(1, reach + 1):
+                pl.when(slab + k < ns)(part_copy(k, j).wait_recv)
+            if j == 0 and direct(ns, nt):
+                for k in (-reach, reach):
+                    @pl.when(inside(slab + k))
+                    def _(k=k):
+                        pl.semaphore_signal(
+                            ready_sem, inc=1, device_id={"slab": slab + k}, device_id_type=MESH)
+            at = pl.ds(j * chunk, chunk)
+            front_c = front_ref[j, pl.ds(0, 3), :]
+            front_t = front_ref[j, pl.ds(3, 1), :]
+            beyond = jnp.concatenate([far_ref[j, c] for c in range(3)], axis=0)
+            beyond = jnp.where(slab + reach < ns, beyond, BACKGROUND)
+            for k in range(reach - 1, 0, -1):
+                pc = near_ref[k - 1, j, pl.ds(0, 3), :]
+                pt = near_ref[k - 1, j, pl.ds(3, 1), :]
+                beyond = jnp.where(slab + k < ns, pc + pt * beyond, beyond)
+            pc = own_ref[j, pl.ds(0, 3), :]
+            pt = own_ref[j, pl.ds(3, 1), :]
+            rendered = front_c + front_t * (pc + pt * beyond)
+            residual = RENDER_WEIGHT * (rendered - target_ref[:, at])
+            color_cot = front_t * residual
+            trans_cot = front_t * jnp.sum(residual * beyond, axis=0, keepdims=True)
+            mask = row_ids16 == row_ref[:, at].astype(jnp.float32).astype(jnp.bfloat16)
+            for c in range(4):
+                cot = color_cot[c:c + 1] if c < 3 else trans_cot
+                top = cot.astype(jnp.bfloat16)
+                low = (cot - top.astype(jnp.float32)).astype(jnp.bfloat16)
+                for half, part in enumerate((top, low)):
+                    spread = jnp.where(mask, part, none)
+                    for q in units:
+                        fresh = j % 2 if c == 0 and half == 0 else None
+                        pltpu.matmul_acc_lhs(
+                            sums_acc[q][c], spread[:, q * WIDTH:(q + 1) * WIDTH], fresh)
+            if j + 1 < chunks:
+                for q in units:
+                    pltpu.matmul_push_rhs(columns(j + 1, q), (j + 1) % 2, q, transpose=True)
         for c in range(4):
-            picked = jnp.where(mask, u[c * step_rows:(c + 1) * step_rows], 0.0)
-            value = jnp.sum(picked, axis=0, keepdims=True)
-            if c == 3:
-                value = jnp.where(behind <= 0, 1.0, value)
-            front_ref[j, pl.ds(c, 1), :] = value
-
-    loads[channels + 3].wait()
-    row_ids16 = row_ids.astype(jnp.float32).astype(jnp.bfloat16)
-    for j in range(chunks):
-        for k in range(1, reach + 1):
-            pl.when(slab + k < ns)(part_copy(k, j).wait_recv)
-        if j == 0 and direct(ns, nt):
-            for k in (-reach, reach):
-                @pl.when(inside(slab + k))
-                def _(k=k):
-                    pl.semaphore_signal(
-                        ready_sem, inc=1, device_id={"slab": slab + k}, device_id_type=MESH)
-        at = pl.ds(j * chunk, chunk)
-        front_c = front_ref[j, pl.ds(0, 3), :]
-        front_t = front_ref[j, pl.ds(3, 1), :]
-        beyond = jnp.concatenate([far_ref[j, c] for c in range(3)], axis=0)
-        beyond = jnp.where(slab + reach < ns, beyond, BACKGROUND)
-        for k in range(reach - 1, 0, -1):
-            pc = near_ref[k - 1, j, pl.ds(0, 3), :]
-            pt = near_ref[k - 1, j, pl.ds(3, 1), :]
-            beyond = jnp.where(slab + k < ns, pc + pt * beyond, beyond)
-        pc = own_ref[j, pl.ds(0, 3), :]
-        pt = own_ref[j, pl.ds(3, 1), :]
-        rendered = front_c + front_t * (pc + pt * beyond)
-        residual = RENDER_WEIGHT * (rendered - target_ref[:, at])
-        color_cot = front_t * residual
-        trans_cot = front_t * jnp.sum(residual * beyond, axis=0, keepdims=True)
-        hot = onehot_ref[:, at]
-        mask = row_ids16 == row_ref[:, at].astype(jnp.float32).astype(jnp.bfloat16)
-        none = jnp.zeros((), jnp.bfloat16)
-        tops = []
-        lows = []
-        for c in range(4):
-            cot = color_cot[c:c + 1] if c < 3 else trans_cot
-            top = cot.astype(jnp.bfloat16)
-            low = (cot - top.astype(jnp.float32)).astype(jnp.bfloat16)
-            tops.append(jnp.where(mask, top, none))
-            lows.append(jnp.where(mask, low, none))
-        u = sum(
-            lax.dot_general(
-                jnp.concatenate(spread, axis=0), hot, (((1,), (1,)), ((), ())),
-                preferred_element_type=jnp.float32)
-            for spread in (tops, lows))
-        if j == 0:
-            table_ref[...] = u
-        else:
-            table_ref[...] += u
+            table_ref[pl.ds(c * rows, rows), :] = sum(pltpu.matmul_pop(sums_acc[q][c]) for q in units)
+
+    pl.run_scoped(scatter, *[
+        pltpu.ACC(q)((rows, WIDTH), jnp.float32) for q in units for _ in range(4)
+    ], *[
+        pltpu.ACC(q)((4 * step_rows, WIDTH), jnp.float32) for _ in range(lags) for q in units
+    ])
 
     zero = jnp.zeros((rx, ry), jnp.float32)
     suffix = [zero, zero, zero]

time: 24.7 us -> 20.5 us (0.83)
  Pallas kernels: 23.9 us -> 19.7 us
    pallas_call x1, Pallas kernels: 22.5 us -> 18.3 us  [per_device(): pl.pallas_call(functools.partial(kernel, ns, nt, chunk), out_shape=(cells...]
where the time goes in v3:
time: 20.5 us; the launch traced here: 20.4 us
  Pallas kernels  19.7 us (96%)
  between operations  0.64 us (3%)
    pallas_call x1, Pallas kernels, per_device(): pl.pallas_call(functools.partial(kernel, ns, nt, chunk), out_shape=(cells...  18.3 us
    pallas_call x1, Pallas kernels, per_device(): pl.pallas_call(adam_kernel, out_shape=(cells, cells, cells), in_specs=[vm...  1.39 us

profile of v3, /device:TPU:0, one launch (start us, length us, event | category | flops | bytes accessed | tf_op | source)
XLA Modules:
  0.0 20.4 jit_solution(3188449873631917827)
XLA Ops:
  0.6 18.3 %render_step.1 = (f32[4,16,8,256]{3,2,1,0:T(8,128)S(1)}, f32[4,16,8,256]{3,2,1,0:T(8,128)S(1)}, f32[4,16,8,256]{3,2,1,0:T(8,128)S(1)}, f32[4,16,8,256]{3,2,1,0:T(8,128)S(1)}, f32[1,128]{1,0:T(1,128)S(1)}) custom-call(f32[4,16,8,256]{3,2,1,0:T(8,128)} %grid_hbm.1, f32[4,16,8,256]{3,2,1,0:T(8,128)} %first_hbm.1, f32[4,16,8,256]{3,2,1,0:T(8,128)} %second_hbm.1, ...), custom_call_target="tpu_custom_call" | custom-call | tf_op jit(solution)/shard_map/render_step/pallas_call | solution.py:445
  19.0 1.4 %adam.1 = (f32[4,16,8,256]{3,2,1,0:T(8,128)}, f32[4,16,8,256]{3,2,1,0:T(8,128)}, f32[4,16,8,256]{3,2,1,0:T(8,128)}) custom-call(f32[4,16,8,256]{3,2,1,0:T(8,128)S(1)} %get-tuple-element.8.grid_ref, f32[4,16,8,256]{3,2,1,0:T(8,128)S(1)} %get-tuple-element.9.first_ref, f32[4,16,8,256]{3,2,1,0:T(8,128)S(1)} %get-tuple-element.10.second_ref, ...), custom_call_target="tpu_custom_call" | custom-call | tf_op jit(solution)/shard_map/adam/pallas_call | solution.py:498

commit v4 on v3

--- a/solution.py
+++ b/solution.py
@@ -20,6 +20,7 @@
 EPSILON = 1e-08
 CHUNK = 512
 WIDTH = 256
+OPENING = 4
 DIRECT_LIMIT = 64
 MESH = pl.DeviceIdType.MESH
 
@@ -78,7 +79,7 @@
     loads += [
         pltpu.make_async_copy(a, b, load_sem.at[channels + i]) for i, (a, b) in enumerate(rest)
     ]
-    for copy in loads:
+    for copy in loads[:-2]:
         copy.start()
 
     barrier = pltpu.get_barrier_semaphore()
@@ -94,6 +95,8 @@
 
     for c in range(channels):
         loads[c].wait()
+    for copy in loads[-2:]:
+        copy.start()
     edge_ref[0] = grid_ref[:, :, rx - 1, :]
     edge_ref[1] = grid_ref[:, :, 0, :]
 
@@ -125,16 +128,11 @@
     pair_ref[:, :ry] = high
     pair_ref[:, ry:] = (full - high.astype(jnp.float32)).astype(jnp.bfloat16)
 
-    pl.semaphore_wait(barrier, greeters)
-
     def whole_copy(k):
         return pltpu.make_async_remote_copy(
             src_ref=whole_ref, dst_ref=wholes_ref.at[k - 1],
             send_sem=whole_send.at[k - 1], recv_sem=whole_recv.at[k - 1],
             device_id=slab_peer(k), device_id_type=MESH)
-
-    for k in range(reach, 0, -1):
-        pl.when(slab + k < ns)(whole_copy(k).start)
 
     def halo_copy(src, dst, i, peer):
         return pltpu.make_async_remote_copy(
@@ -147,9 +145,6 @@
         (halo_copy(edge_ref.at[0], xhalo_ref.at[0], 2, tile_peer(1)), tile < nt - 1, tile > 0),
         (halo_copy(edge_ref.at[1], xhalo_ref.at[1], 3, tile_peer(nt - 1)), tile > 0, tile < nt - 1),
     ]
-    for copy, sends, _ in halos:
-        pl.when(sends)(copy.start)
-
     def part_copy(k, j):
         src, dst = (last_ref, far_ref) if k == reach else (own_ref, near_ref.at[k - 1])
         return pltpu.make_async_remote_copy(
@@ -163,6 +158,15 @@
     for copy in loads[channels:channels + 3]:
         copy.wait()
     units = range(chunk // WIDTH)
+
+    def enter():
+        pl.semaphore_wait(barrier, greeters)
+        for k in range(reach, 0, -1):
+            pl.when(slab + k < ns)(whole_copy(k).start)
+        for copy, sends, _ in halos[2:]:
+            pl.when(sends)(copy.start)
+
+    opening = min(OPENING, chunks)
 
     def gather(*accs):
         banks = [[accs[(b * len(units) + q) * 4:][:4] for q in units] for b in range(2)]
@@ -200,22 +204,27 @@
                 own_ref[i, pl.ds(c, 1), :] = part
             for c in range(3):
                 last_ref[i, c] = own_ref[i, pl.ds(c, 1), :] + BACKGROUND * part
-            for k in range(1, reach + 1):
-                pl.when(slab >= k)(part_copy(k, i).start)
+            if j < opening:
+                continue
+            if j == opening:
+                enter()
+            for n in range(0 if j == opening else i, j):
+                for k in range(1, reach + 1):
+                    pl.when(slab >= k)(part_copy(k, n).start)
 
     pl.run_scoped(gather, *[
         pltpu.ACC(q)((rows, WIDTH), jnp.float32)
         for _ in range(2) for q in units for _ in range(4)
     ])
 
-    for copy, _, receives in halos:
-        pl.when(receives)(copy.wait_recv)
+    for copy, sends, _ in halos[:2]:
+        pl.when(sends)(copy.start)
     x_ids = lax.broadcasted_iota(jnp.int32, (rx, ry), 0)
     lane_ids = lax.broadcasted_iota(jnp.int32, (rx, ry), 1)
     first_x = tile == 0
     last_x = tile == nt - 1
-    for c in range(channels):
-        for z in range(depth):
+    def smooth_planes(c, planes):
+        for z in planes:
             g = grid_ref[c, z]
             if z > 0:
                 below = grid_ref[c, z - 1]
@@ -256,6 +265,7 @@
     row_ids16 = row_ids.astype(jnp.float32).astype(jnp.bfloat16)
     none = jnp.zeros((), jnp.bfloat16)
     lags = 4
+    inner = min(channels, chunks)
 
     def scatter(*accs):
         sums_acc = [accs[q * 4:][:4] for q in units]
@@ -288,6 +298,9 @@
         for j in range(chunks):
             for k in range(1, reach + 1):
                 pl.when(slab + k < ns)(part_copy(k, j).wait_recv)
+            if j == chunks - inner:
+                for copy, _, receives in halos[2:]:
+                    pl.when(receives)(copy.wait_recv)
             if j == 0 and direct(ns, nt):
                 for k in (-reach, reach):
                     @pl.when(inside(slab + k))
@@ -323,6 +336,13 @@
             if j + 1 < chunks:
                 for q in units:
                     pltpu.matmul_push_rhs(columns(j + 1, q), (j + 1) % 2, q, transpose=True)
+            if j >= chunks - inner:
+                for c in range((j - chunks + inner) * channels // inner, (j + 1 - chunks + inner) * channels // inner):
+                    smooth_planes(c, range(1, depth - 1))
+        for copy, _, receives in halos[:2]:
+            pl.when(receives)(copy.wait_recv)
+        for c in range(channels):
+            smooth_planes(c, (0, depth - 1) if depth > 1 else (0,))
         for c in range(4):
             table_ref[pl.ds(c * rows, rows), :] = sum(pltpu.matmul_pop(sums_acc[q][c]) for q in units)
 

time: 20.5 us -> 21.1 us (1.029)
  Pallas kernels: 19.7 us -> 20.3 us
    pallas_call x1, Pallas kernels: 18.3 us -> 18.9 us  [per_device(): pl.pallas_call(functools.partial(kernel, ns, nt, chunk), out_shape=(cells...]
where the time goes in v4:
time: 21.1 us; the launch traced here: 21 us
  Pallas kernels  20.3 us (96%)
  between operations  0.64 us (3%)
    pallas_call x1, Pallas kernels, per_device(): pl.pallas_call(functools.partial(kernel, ns, nt, chunk), out_shape=(cells...  18.9 us
    pallas_call x1, Pallas kernels, per_device(): pl.pallas_call(adam_kernel, out_shape=(cells, cells, cells), in_specs=[vm...  1.39 us

profile of v4, /device:TPU:0, one launch (start us, length us, event | category | flops | bytes accessed | tf_op | source)
XLA Modules:
  0.0 21.0 jit_solution(8788194368633451105)
XLA Ops:
  0.6 18.9 %render_step.1 = (f32[4,16,8,256]{3,2,1,0:T(8,128)S(1)}, f32[4,16,8,256]{3,2,1,0:T(8,128)S(1)}, f32[4,16,8,256]{3,2,1,0:T(8,128)S(1)}, f32[4,16,8,256]{3,2,1,0:T(8,128)S(1)}, f32[1,128]{1,0:T(1,128)S(1)}) custom-call(f32[4,16,8,256]{3,2,1,0:T(8,128)} %grid_hbm.1, f32[4,16,8,256]{3,2,1,0:T(8,128)} %first_hbm.1, f32[4,16,8,256]{3,2,1,0:T(8,128)} %second_hbm.1, ...), custom_call_target="tpu_custom_call" | custom-call | tf_op jit(solution)/shard_map/render_step/pallas_call | solution.py:465
  19.6 1.4 %adam.1 = (f32[4,16,8,256]{3,2,1,0:T(8,128)}, f32[4,16,8,256]{3,2,1,0:T(8,128)}, f32[4,16,8,256]{3,2,1,0:T(8,128)}) custom-call(f32[4,16,8,256]{3,2,1,0:T(8,128)S(1)} %get-tuple-element.8.grid_ref, f32[4,16,8,256]{3,2,1,0:T(8,128)S(1)} %get-tuple-element.9.first_ref, f32[4,16,8,256]{3,2,1,0:T(8,128)S(1)} %get-tuple-element.10.second_ref, ...), custom_call_target="tpu_custom_call" | custom-call | tf_op jit(solution)/shard_map/adam/pallas_call | solution.py:518

commit v5 on v4

--- a/solution.py
+++ b/solution.py
@@ -20,7 +20,7 @@
 EPSILON = 1e-08
 CHUNK = 512
 WIDTH = 256
-OPENING = 4
+OPENING = 1
 DIRECT_LIMIT = 64
 MESH = pl.DeviceIdType.MESH
 
@@ -52,13 +52,10 @@
         return {"tile": lax.rem(tile + d, nt)}
 
     if direct(ns, nt):
-        pair = {"tile": tile + 1 - 2 * lax.rem(tile, 2)}
-        half = nt // 2
-        others = [
-            {"slab": lax.rem(slab + k // half, ns), "tile": lax.rem(tile + 2 * (k % half), nt)}
-            for k in range(1, ns * half)
-        ]
-        phases = [[pair], others]
+        phases = [[
+            {"slab": lax.rem(slab + k // nt, ns), "tile": lax.rem(tile + k % nt, nt)}
+            for k in range(1, ns * nt)
+        ]]
         near = reach
     else:
         phases = [[tile_peer(d) for d in range(1, nt)], [slab_peer(d) for d in range(1, ns)]]
@@ -376,34 +373,36 @@
 
     local = jnp.sum(squares)
 
-    def norm_copy(phase, slot, peer):
+    def norm_copy(phase, slots, peer=None):
+        src = nsend_ref.at[pl.ds(phase, 1)] if peer else nrecv_ref.at[slots]
         return pltpu.make_async_remote_copy(
-            src_ref=nsend_ref.at[phase], dst_ref=nrecv_ref.at[slot],
-            send_sem=norm_send.at[slot], recv_sem=norm_recv.at[slot],
-            device_id=peer, device_id_type=MESH)
+            src_ref=src, dst_ref=nrecv_ref.at[slots],
+            send_sem=norm_send.at[phase], recv_sem=norm_recv.at[phase],
+            device_id=peer or tile_peer(1), device_id_type=MESH)
 
     if direct(ns, nt):
         far = inside(slab - reach).astype(jnp.int32) + inside(slab + reach).astype(jnp.int32)
         pl.semaphore_wait(ready_sem, far)
     value = jnp.full((1, 128), local, jnp.float32)
-    copies = []
     base = 0
     for phase, peers in enumerate(phases):
         nsend_ref[phase] = value
-        group = [norm_copy(phase, base + i, peer) for i, peer in enumerate(peers)]
-        for copy in group:
-            copy.start()
-        for i, copy in enumerate(group):
-            copy.wait_recv()
-            value = value + nrecv_ref[base + i]
-        base += len(group)
-        copies += group
+        for i, peer in enumerate(peers):
+            norm_copy(phase, pl.ds(base + i, 1), peer).start()
+        if phase == 0:
+            for copy in loads[-2:]:
+                copy.wait()
+            first_ref[...] = BETA_ONE * first_ref[...]
+            second_ref[...] = BETA_TWO * second_ref[...]
+        norm_copy(phase, pl.ds(base, len(peers))).wait_recv()
+        value = value + jnp.sum(nrecv_ref[pl.ds(base, len(peers)), 0, :], axis=0, keepdims=True)
+        base += len(peers)
     limit = CLIP_RMS * math.sqrt(4.0 * total_depth * (rx * nt) * ry)
     scale_ref[...] = limit / jnp.maximum(jnp.sqrt(value), limit)
-    for copy in loads[channels + 4:]:
-        copy.wait()
-    for copy in copies:
-        copy.wait_send()
+    base = 0
+    for phase, peers in enumerate(phases):
+        norm_copy(phase, pl.ds(base, len(peers))).wait_send()
+        base += len(peers)
     for copy, sends, _ in halos:
         pl.when(sends)(copy.wait_send)
     for j in range(chunks):
@@ -418,7 +417,7 @@
 
 
 def direct(ns, nt):
-    return ns * nt <= DIRECT_LIMIT and nt % 2 == 0
+    return ns * nt <= DIRECT_LIMIT
 
 
 def adam_kernel(
@@ -426,24 +425,31 @@
     grid_hbm, first_hbm, second_hbm, grid_out, first_out, second_out, sem,
 ):
     channels, depth, rx, ry = grid_ref.shape
+    gain = (1.0 - BETA_ONE**STEP) / LEARN_RATE
+    slope = gain / math.sqrt(1.0 - BETA_TWO**STEP)
+    offset = gain * EPSILON
     scale = jnp.broadcast_to(scale_ref[0:1, 0:1], (rx, ry))
+    linear = (1.0 - BETA_ONE) * scale
+    square = (1.0 - BETA_TWO) * scale * scale
     copies = []
+    pieces = 2 if depth % 2 == 0 else 1
     for c in range(channels):
-        for z in range(depth):
-            clipped = grad_ref[c, z] * scale
-            first = BETA_ONE * first_ref[c, z] + (1.0 - BETA_ONE) * clipped
-            second = BETA_TWO * second_ref[c, z] + (1.0 - BETA_TWO) * clipped * clipped
-            first_out[c, z] = first
-            second_out[c, z] = second
-            first_hat = first * (1.0 / (1.0 - BETA_ONE**STEP))
-            second_hat = second * (1.0 / (1.0 - BETA_TWO**STEP))
-            grid_out[c, z] = grid_ref[c, z] - LEARN_RATE * first_hat / (
-                jnp.sqrt(second_hat) + EPSILON)
-        pairs = ((first_out, first_hbm), (second_out, second_hbm), (grid_out, grid_hbm))
-        for i, (a, b) in enumerate(pairs):
-            copy = pltpu.make_async_copy(a.at[c], b.at[c], sem.at[i, c])
-            copy.start()
-            copies.append(copy)
+        for p in range(pieces):
+            planes = range(p * depth // pieces, (p + 1) * depth // pieces)
+            for z in planes:
+                g = grad_ref[c, z]
+                first = first_ref[c, z] + linear * g
+                second = second_ref[c, z] + square * g * g
+                first_out[c, z] = first
+                second_out[c, z] = second
+                root = second * lax.rsqrt(second)
+                grid_out[c, z] = grid_ref[c, z] - first / (root * slope + offset)
+            at = pl.ds(p * depth // pieces, depth // pieces)
+            pairs = ((first_out, first_hbm), (second_out, second_hbm), (grid_out, grid_hbm))
+            for i, (a, b) in enumerate(pairs):
+                copy = pltpu.make_async_copy(a.at[c, at], b.at[c, at], sem.at[i, c, p])
+                copy.start()
+                copies.append(copy)
     for copy in copies:
         copy.wait()
 
@@ -457,7 +463,7 @@
     chunks = rays // chunk
     rows = depth * rx
     reach = span_reach(ns)
-    messages = ns * nt // 2 if direct(ns, nt) else nt + ns - 2
+    messages = ns * nt - 1 if direct(ns, nt) else nt + ns - 2
     f32 = jnp.float32
     vmem = pl.BlockSpec(memory_space=pltpu.VMEM)
     hbm = pl.BlockSpec(memory_space=pltpu.HBM)
@@ -498,8 +504,8 @@
             pltpu.SemaphoreType.REGULAR,
             pltpu.SemaphoreType.DMA((4,)),
             pltpu.SemaphoreType.DMA((4,)),
-            pltpu.SemaphoreType.DMA((messages,)),
-            pltpu.SemaphoreType.DMA((messages,)),
+            pltpu.SemaphoreType.DMA((2,)),
+            pltpu.SemaphoreType.DMA((2,)),
             pltpu.SemaphoreType.DMA((channels + 6,)),
         ],
         compiler_params=pltpu.CompilerParams(
@@ -524,7 +530,7 @@
             pltpu.VMEM(voxel_grid.shape, f32),
             pltpu.VMEM(voxel_grid.shape, f32),
             pltpu.VMEM(voxel_grid.shape, f32),
-            pltpu.SemaphoreType.DMA((3, channels)),
+            pltpu.SemaphoreType.DMA((3, channels, 2)),
         ],
         compiler_params=pltpu.CompilerParams(vmem_limit_bytes=32 * 1024 * 1024),
         name="adam",

time: 21.1 us -> 20 us (0.948)
  Pallas kernels: 20.3 us -> 19.2 us
    pallas_call x1, Pallas kernels: 18.9 us -> 17.8 us  [per_device(): pl.pallas_call(functools.partial(kernel, ns, nt, chunk), out_shape=(cells...]
where the time goes in v5:
time: 20 us; the launch traced here: 19.8 us
  Pallas kernels  19.2 us (96%)
  between operations  0.64 us (3%)
    pallas_call x1, Pallas kernels, per_device(): pl.pallas_call(functools.partial(kernel, ns, nt, chunk), out_shape=(cells...  17.8 us
    pallas_call x1, Pallas kernels, per_device(): pl.pallas_call(adam_kernel, out_shape=(cells, cells, cells), in_specs=[vm...  1.41 us

profile of v5, /device:TPU:0, one launch (start us, length us, event | category | flops | bytes accessed | tf_op | source)
XLA Modules:
  0.0 19.8 jit_solution(12903744640386800728)
XLA Ops:
  0.6 17.8 %render_step.1 = (f32[4,16,8,256]{3,2,1,0:T(8,128)S(1)}, f32[4,16,8,256]{3,2,1,0:T(8,128)S(1)}, f32[4,16,8,256]{3,2,1,0:T(8,128)S(1)}, f32[4,16,8,256]{3,2,1,0:T(8,128)S(1)}, f32[1,128]{1,0:T(1,128)S(1)}) custom-call(f32[4,16,8,256]{3,2,1,0:T(8,128)} %grid_hbm.1, f32[4,16,8,256]{3,2,1,0:T(8,128)} %first_hbm.1, f32[4,16,8,256]{3,2,1,0:T(8,128)} %second_hbm.1, ...), custom_call_target="tpu_custom_call" | custom-call | tf_op jit(solution)/shard_map/render_step/pallas_call | solution.py:471
  18.4 1.4 %adam.1 = (f32[4,16,8,256]{3,2,1,0:T(8,128)}, f32[4,16,8,256]{3,2,1,0:T(8,128)}, f32[4,16,8,256]{3,2,1,0:T(8,128)}) custom-call(f32[4,16,8,256]{3,2,1,0:T(8,128)S(1)} %get-tuple-element.8.grid_ref, f32[4,16,8,256]{3,2,1,0:T(8,128)S(1)} %get-tuple-element.9.first_ref, f32[4,16,8,256]{3,2,1,0:T(8,128)S(1)} %get-tuple-element.10.second_ref, ...), custom_call_target="tpu_custom_call" | custom-call | tf_op jit(solution)/shard_map/adam/pallas_call | solution.py:524

commit v6 on v5

--- a/solution.py
+++ b/solution.py
@@ -21,6 +21,7 @@
 CHUNK = 512
 WIDTH = 256
 OPENING = 1
+PIECES = 4
 DIRECT_LIMIT = 64
 MESH = pl.DeviceIdType.MESH
 
@@ -29,14 +30,15 @@
     ns, nt, chunk,
     grid_hbm, first_hbm, second_hbm, pix_hbm, start_hbm, count_hbm, target_hbm,
     grid_ref, first_ref, second_ref, grad_ref, scale_ref,
-    pix_ref, start_ref, count_ref, target_ref,
+    ints_ref, target_ref,
     pair_ref, trans_ref, weight_ref, sig_ref, onehot_ref, row_ref, table_ref,
-    whole_ref, wholes_ref, front_ref, own_ref, last_ref, near_ref, far_ref,
+    whole_ref, wholes_ref, front_ref, own_ref, last_ref, far_ref,
     edge_ref, xhalo_ref, zhalo_ref, nsend_ref, nrecv_ref,
-    whole_send, whole_recv, part_send, part_recv, ready_sem, halo_send, halo_recv, norm_send, norm_recv, load_sem,
+    whole_sem, part_send, part_recv, ready_sem, halo_send, halo_recv, norm_send, norm_recv, load_sem,
 ):
     channels, depth, rx, ry = grid_ref.shape
-    rays = pix_ref.shape[1]
+    rays = ints_ref.shape[2]
+    pix_ref, start_ref, count_ref = (ints_ref.at[i] for i in range(3))
     chunks = rays // chunk
     total_depth = depth * ns
     reach = span_reach(ns)
@@ -65,19 +67,22 @@
     def inside(s):
         return (s >= 0) & (s < ns)
 
-    loads = [
-        pltpu.make_async_copy(grid_hbm.at[c], grid_ref.at[c], load_sem.at[c])
-        for c in range(channels)
+    pieces = split(depth)
+    step = depth // pieces
+    grid_load = pltpu.make_async_copy(grid_hbm, grid_ref, load_sem.at[0])
+    for c in range(channels):
+        for p in range(pieces):
+            at = pl.ds(p * step, step)
+            pltpu.make_async_copy(grid_hbm.at[c, at], grid_ref.at[c, at], load_sem.at[0]).start()
+    for i, a in enumerate((pix_hbm, start_hbm, count_hbm)):
+        pltpu.make_async_copy(a, ints_ref.at[i], load_sem.at[1]).start()
+    ints_load = pltpu.make_async_copy(ints_ref, ints_ref, load_sem.at[1])
+    target_load = pltpu.make_async_copy(target_hbm, target_ref, load_sem.at[2])
+    target_load.start()
+    moment_loads = [
+        pltpu.make_async_copy(first_hbm, first_ref, load_sem.at[3]),
+        pltpu.make_async_copy(second_hbm, second_ref, load_sem.at[4]),
     ]
-    rest = (
-        (pix_hbm, pix_ref), (start_hbm, start_ref), (count_hbm, count_ref),
-        (target_hbm, target_ref), (first_hbm, first_ref), (second_hbm, second_ref),
-    )
-    loads += [
-        pltpu.make_async_copy(a, b, load_sem.at[channels + i]) for i, (a, b) in enumerate(rest)
-    ]
-    for copy in loads[:-2]:
-        copy.start()
 
     barrier = pltpu.get_barrier_semaphore()
     for d in range(1, nt):
@@ -90,9 +95,8 @@
                 barrier, inc=1, device_id={"slab": slab + k}, device_id_type=MESH)
         greeters = greeters + inside(slab + k).astype(jnp.int32)
 
-    for c in range(channels):
-        loads[c].wait()
-    for copy in loads[-2:]:
+    grid_load.wait()
+    for copy in moment_loads:
         copy.start()
     edge_ref[0] = grid_ref[:, :, rx - 1, :]
     edge_ref[1] = grid_ref[:, :, 0, :]
@@ -125,42 +129,59 @@
     pair_ref[:, :ry] = high
     pair_ref[:, ry:] = (full - high.astype(jnp.float32)).astype(jnp.bfloat16)
 
+    def waiter(ref, sem):
+        return pltpu.make_async_remote_copy(
+            src_ref=ref, dst_ref=ref, send_sem=sem, recv_sem=sem,
+            device_id=tile_peer(1), device_id_type=MESH)
+
+    def wait_sent(ref, sem, count, most):
+        for n in range(1, most + 1):
+            pl.when(count == n)(waiter(ref.at[pl.ds(0, n)], sem).wait_send)
+
+    def wait_received(ref, sem, count, most):
+        for n in range(1, most + 1):
+            pl.when(count == n)(waiter(ref.at[pl.ds(0, n)], sem).wait_recv)
+
+    behind_count = jnp.minimum(slab, reach)
+    ahead_count = jnp.minimum(ns - 1 - slab, reach)
+    beside_count = (tile < nt - 1).astype(jnp.int32) + (tile > 0).astype(jnp.int32)
+    level_count = (slab < ns - 1).astype(jnp.int32) + (slab > 0).astype(jnp.int32)
+
     def whole_copy(k):
         return pltpu.make_async_remote_copy(
             src_ref=whole_ref, dst_ref=wholes_ref.at[k - 1],
-            send_sem=whole_send.at[k - 1], recv_sem=whole_recv.at[k - 1],
+            send_sem=whole_sem.at[0], recv_sem=whole_sem.at[1],
             device_id=slab_peer(k), device_id_type=MESH)
 
     def halo_copy(src, dst, i, peer):
         return pltpu.make_async_remote_copy(
-            src_ref=src, dst_ref=dst, send_sem=halo_send.at[i], recv_sem=halo_recv.at[i],
+            src_ref=src, dst_ref=dst, send_sem=halo_send.at[i // 2], recv_sem=halo_recv.at[i // 2],
             device_id=peer, device_id_type=MESH)
 
     halos = [
-        (halo_copy(grid_ref.at[:, depth - 1], zhalo_ref.at[0], 0, slab_peer(1)), slab < ns - 1, slab > 0),
-        (halo_copy(grid_ref.at[:, 0], zhalo_ref.at[1], 1, slab_peer(ns - 1)), slab > 0, slab < ns - 1),
-        (halo_copy(edge_ref.at[0], xhalo_ref.at[0], 2, tile_peer(1)), tile < nt - 1, tile > 0),
-        (halo_copy(edge_ref.at[1], xhalo_ref.at[1], 3, tile_peer(nt - 1)), tile > 0, tile < nt - 1),
+        (halo_copy(grid_ref.at[:, depth - 1], zhalo_ref.at[0], 0, slab_peer(1)), slab < ns - 1),
+        (halo_copy(grid_ref.at[:, 0], zhalo_ref.at[1], 1, slab_peer(ns - 1)), slab > 0),
+        (halo_copy(edge_ref.at[0], xhalo_ref.at[0], 2, tile_peer(1)), tile < nt - 1),
+        (halo_copy(edge_ref.at[1], xhalo_ref.at[1], 3, tile_peer(nt - 1)), tile > 0),
     ]
     def part_copy(k, j):
-        src, dst = (last_ref, far_ref) if k == reach else (own_ref, near_ref.at[k - 1])
+        src = last_ref if k == reach else own_ref
         return pltpu.make_async_remote_copy(
-            src_ref=src.at[j], dst_ref=dst.at[j],
-            send_sem=part_send.at[k - 1, j], recv_sem=part_recv.at[k - 1, j],
+            src_ref=src.at[j], dst_ref=far_ref.at[j, pl.ds(4 * (k - 1), src.shape[1])],
+            send_sem=part_send.at[k - 1], recv_sem=part_recv.at[j],
             device_id=slab_peer(ns - k), device_id_type=MESH)
 
     y_ids = lax.broadcasted_iota(jnp.int32, (ry, chunk), 0).astype(jnp.float32).astype(jnp.bfloat16)
     row_ids = lax.broadcasted_iota(jnp.int32, (rows, chunk), 0)
 
-    for copy in loads[channels:channels + 3]:
-        copy.wait()
+    ints_load.wait()
     units = range(chunk // WIDTH)
 
     def enter():
         pl.semaphore_wait(barrier, greeters)
         for k in range(reach, 0, -1):
             pl.when(slab + k < ns)(whole_copy(k).start)
-        for copy, sends, _ in halos[2:]:
+        for copy, sends in halos[2:]:
             pl.when(sends)(copy.start)
 
     opening = min(OPENING, chunks)
@@ -198,9 +219,9 @@
                 part = jnp.sum(jnp.where(mask, u, 0.0), axis=0, keepdims=True)
                 if c == 3:
                     part = jnp.where(row < 0, 1.0, part)
-                own_ref[i, pl.ds(c, 1), :] = part
+                own_ref[i, c] = part
             for c in range(3):
-                last_ref[i, c] = own_ref[i, pl.ds(c, 1), :] + BACKGROUND * part
+                last_ref[i, c] = own_ref[i, c] + BACKGROUND * part
             if j < opening:
                 continue
             if j == opening:
@@ -214,7 +235,7 @@
         for _ in range(2) for q in units for _ in range(4)
     ])
 
-    for copy, sends, _ in halos[:2]:
+    for copy, sends in halos[:2]:
         pl.when(sends)(copy.start)
     x_ids = lax.broadcasted_iota(jnp.int32, (rx, ry), 0)
     lane_ids = lax.broadcasted_iota(jnp.int32, (rx, ry), 1)
@@ -242,8 +263,7 @@
             smooth = (g - below) + (g - above) + (g - left) + (g - right) + (g - down) + (g - up)
             grad_ref[c, z] = (2.0 * TV_WEIGHT) * smooth
 
-    for k in range(1, reach + 1):
-        pl.when(slab >= k)(whole_copy(k).wait_recv)
+    wait_received(wholes_ref, whole_sem.at[1], behind_count, reach)
     folded = [[] for _ in range(4)]
     fold_t = jnp.ones((rx, ry), jnp.float32)
     fold_c = [jnp.zeros((rx, ry), jnp.float32)] * 3
@@ -289,15 +309,15 @@
                     value = jnp.where(behind <= 0, 1.0, value)
                 front_ref[j, pl.ds(c, 1), :] = value
 
-        loads[channels + 3].wait()
+        target_load.wait()
         for q in units:
             pltpu.matmul_push_rhs(columns(0, q), 0, q, transpose=True)
         for j in range(chunks):
-            for k in range(1, reach + 1):
-                pl.when(slab + k < ns)(part_copy(k, j).wait_recv)
+            for n in range(1, reach + 1):
+                size = far_ref.shape[1] if n == reach else 4 * n
+                pl.when(ahead_count == n)(waiter(far_ref.at[j, pl.ds(0, size)], part_recv.at[j]).wait_recv)
             if j == chunks - inner:
-                for copy, _, receives in halos[2:]:
-                    pl.when(receives)(copy.wait_recv)
+                wait_received(xhalo_ref, halo_recv.at[1], beside_count, 2)
             if j == 0 and direct(ns, nt):
                 for k in (-reach, reach):
                     @pl.when(inside(slab + k))
@@ -307,14 +327,14 @@
             at = pl.ds(j * chunk, chunk)
             front_c = front_ref[j, pl.ds(0, 3), :]
             front_t = front_ref[j, pl.ds(3, 1), :]
-            beyond = jnp.concatenate([far_ref[j, c] for c in range(3)], axis=0)
+            beyond = far_ref[j, pl.ds(4 * (reach - 1), 3), 0, :]
             beyond = jnp.where(slab + reach < ns, beyond, BACKGROUND)
             for k in range(reach - 1, 0, -1):
-                pc = near_ref[k - 1, j, pl.ds(0, 3), :]
-                pt = near_ref[k - 1, j, pl.ds(3, 1), :]
+                pc = far_ref[j, pl.ds(4 * (k - 1), 3), 0, :]
+                pt = far_ref[j, 4 * k - 1]
                 beyond = jnp.where(slab + k < ns, pc + pt * beyond, beyond)
-            pc = own_ref[j, pl.ds(0, 3), :]
-            pt = own_ref[j, pl.ds(3, 1), :]
+            pc = own_ref[j, pl.ds(0, 3), 0, :]
+            pt = own_ref[j, 3]
             rendered = front_c + front_t * (pc + pt * beyond)
             residual = RENDER_WEIGHT * (rendered - target_ref[:, at])
             color_cot = front_t * residual
@@ -336,8 +356,7 @@
             if j >= chunks - inner:
                 for c in range((j - chunks + inner) * channels // inner, (j + 1 - chunks + inner) * channels // inner):
                     smooth_planes(c, range(1, depth - 1))
-        for copy, _, receives in halos[:2]:
-            pl.when(receives)(copy.wait_recv)
+        wait_received(zhalo_ref, halo_recv.at[0], level_count, 2)
         for c in range(channels):
             smooth_planes(c, (0, depth - 1) if depth > 1 else (0,))
         for c in range(4):
@@ -390,10 +409,16 @@
         for i, peer in enumerate(peers):
             norm_copy(phase, pl.ds(base + i, 1), peer).start()
         if phase == 0:
-            for copy in loads[-2:]:
+            for copy in moment_loads:
                 copy.wait()
             first_ref[...] = BETA_ONE * first_ref[...]
             second_ref[...] = BETA_TWO * second_ref[...]
+            wait_sent(zhalo_ref, halo_send.at[0], level_count, 2)
+            wait_sent(edge_ref, halo_send.at[1], beside_count, 2)
+            wait_sent(wholes_ref, whole_sem.at[0], ahead_count, reach)
+            for k in range(1, reach + 1):
+                src = last_ref if k == reach else own_ref
+                pl.when(slab >= k)(waiter(src, part_send.at[k - 1]).wait_send)
         norm_copy(phase, pl.ds(base, len(peers))).wait_recv()
         value = value + jnp.sum(nrecv_ref[pl.ds(base, len(peers)), 0, :], axis=0, keepdims=True)
         base += len(peers)
@@ -403,13 +428,10 @@
     for phase, peers in enumerate(phases):
         norm_copy(phase, pl.ds(base, len(peers))).wait_send()
         base += len(peers)
-    for copy, sends, _ in halos:
-        pl.when(sends)(copy.wait_send)
-    for j in range(chunks):
-        for k in range(1, reach + 1):
-            pl.when(slab >= k)(part_copy(k, j).wait_send)
-    for k in range(1, reach + 1):
-        pl.when(slab + k < ns)(whole_copy(k).wait_send)
+
+
+def split(depth):
+    return math.gcd(depth, PIECES)
 
 
 def span_reach(ns):
@@ -431,8 +453,8 @@
     scale = jnp.broadcast_to(scale_ref[0:1, 0:1], (rx, ry))
     linear = (1.0 - BETA_ONE) * scale
     square = (1.0 - BETA_TWO) * scale * scale
-    copies = []
-    pieces = 2 if depth % 2 == 0 else 1
+    pairs = ((first_out, first_hbm), (second_out, second_hbm), (grid_out, grid_hbm))
+    pieces = split(depth)
     for c in range(channels):
         for p in range(pieces):
             planes = range(p * depth // pieces, (p + 1) * depth // pieces)
@@ -445,13 +467,10 @@
                 root = second * lax.rsqrt(second)
                 grid_out[c, z] = grid_ref[c, z] - first / (root * slope + offset)
             at = pl.ds(p * depth // pieces, depth // pieces)
-            pairs = ((first_out, first_hbm), (second_out, second_hbm), (grid_out, grid_hbm))
             for i, (a, b) in enumerate(pairs):
-                copy = pltpu.make_async_copy(a.at[c, at], b.at[c, at], sem.at[i, c, p])
-                copy.start()
-                copies.append(copy)
-    for copy in copies:
-        copy.wait()
+                pltpu.make_async_copy(a.at[c, at], b.at[c, at], sem.at[i]).start()
+    for i, (a, b) in enumerate(pairs):
+        pltpu.make_async_copy(a, b, sem.at[i]).wait()
 
 
 def per_device(voxel_grid, first_moment, second_moment, pixel_index, start_slab, ray_count, target):
@@ -463,6 +482,7 @@
     chunks = rays // chunk
     rows = depth * rx
     reach = span_reach(ns)
+    phases = 1 if direct(ns, nt) else 2
     messages = ns * nt - 1 if direct(ns, nt) else nt + ns - 2
     f32 = jnp.float32
     vmem = pl.BlockSpec(memory_space=pltpu.VMEM)
@@ -474,9 +494,7 @@
         in_specs=[hbm] * 7,
         out_specs=(vmem,) * 5,
         scratch_shapes=[
-            pltpu.VMEM((1, rays), jnp.int32),
-            pltpu.VMEM((1, rays), jnp.int32),
-            pltpu.VMEM((1, rays), jnp.int32),
+            pltpu.VMEM((3, 1, rays), jnp.int32),
             pltpu.VMEM(target.shape, f32),
             pltpu.VMEM((channels * rows, 2 * ry), jnp.bfloat16),
             pltpu.VMEM((depth, rx, ry), f32),
@@ -488,25 +506,23 @@
             pltpu.VMEM((4, rx, ry), f32),
             pltpu.VMEM((reach, 4, rx, ry), f32),
             pltpu.VMEM((chunks, 4, chunk), f32),
-            pltpu.VMEM((chunks, 4, chunk), f32),
+            pltpu.VMEM((chunks, 4, 1, chunk), f32),
             pltpu.VMEM((chunks, 3, 1, chunk), f32),
-            pltpu.VMEM((max(reach - 1, 1), chunks, 4, chunk), f32),
-            pltpu.VMEM((chunks, 3, 1, chunk), f32),
+            pltpu.VMEM((chunks, 4 * reach - 1, 1, chunk), f32),
             pltpu.VMEM((2, channels, depth, ry), f32),
             pltpu.VMEM((2, channels, depth, ry), f32),
             pltpu.VMEM((2, channels, rx, ry), f32),
             pltpu.VMEM((2, 1, 128), f32),
             pltpu.VMEM((messages, 1, 128), f32),
+            pltpu.SemaphoreType.DMA((2,)),
             pltpu.SemaphoreType.DMA((reach,)),
-            pltpu.SemaphoreType.DMA((reach,)),
-            pltpu.SemaphoreType.DMA((reach, chunks)),
-            pltpu.SemaphoreType.DMA((reach, chunks)),
+            pltpu.SemaphoreType.DMA((chunks,)),
             pltpu.SemaphoreType.REGULAR,
-            pltpu.SemaphoreType.DMA((4,)),
-            pltpu.SemaphoreType.DMA((4,)),
             pltpu.SemaphoreType.DMA((2,)),
             pltpu.SemaphoreType.DMA((2,)),
-            pltpu.SemaphoreType.DMA((channels + 6,)),
+            pltpu.SemaphoreType.DMA((phases,)),
+            pltpu.SemaphoreType.DMA((phases,)),
+            pltpu.SemaphoreType.DMA((5,)),
         ],
         compiler_params=pltpu.CompilerParams(
             collective_id=0, has_side_effects=True, vmem_limit_bytes=32 * 1024 * 1024
@@ -530,7 +546,7 @@
             pltpu.VMEM(voxel_grid.shape, f32),
             pltpu.VMEM(voxel_grid.shape, f32),
             pltpu.VMEM(voxel_grid.shape, f32),
-            pltpu.SemaphoreType.DMA((3, channels, 2)),
+            pltpu.SemaphoreType.DMA((3,)),
         ],
         compiler_params=pltpu.CompilerParams(vmem_limit_bytes=32 * 1024 * 1024),
         name="adam",

time: 20 us -> 19.5 us (0.975)
  Pallas kernels: 19.2 us -> 18.7 us
    pallas_call x1, Pallas kernels: 17.8 us -> 17.4 us  [per_device(): pl.pallas_call(functools.partial(kernel, ns, nt, chunk), out_shape=(cells...]
    pallas_call x1, Pallas kernels: 1.41 us -> 1.21 us  [per_device(): pl.pallas_call(adam_kernel, out_shape=(cells, cells, cells), in_specs=[vm...]
where the time goes in v6:
time: 19.5 us; the launch traced here: 19.3 us
  Pallas kernels  18.7 us (96%)
  between operations  0.64 us (3%)
    pallas_call x1, Pallas kernels, per_device(): pl.pallas_call(functools.partial(kernel, ns, nt, chunk), out_shape=(cells...  17.4 us
    pallas_call x1, Pallas kernels, per_device(): pl.pallas_call(adam_kernel, out_shape=(cells, cells, cells), in_specs=[vm...  1.21 us

profile of v6, /device:TPU:0, one launch (start us, length us, event | category | flops | bytes accessed | tf_op | source)
XLA Modules:
  0.0 19.3 jit_solution(16008831324162804049)
XLA Ops:
  0.6 17.4 %render_step.1 = (f32[4,16,8,256]{3,2,1,0:T(8,128)S(1)}, f32[4,16,8,256]{3,2,1,0:T(8,128)S(1)}, f32[4,16,8,256]{3,2,1,0:T(8,128)S(1)}, f32[4,16,8,256]{3,2,1,0:T(8,128)S(1)}, f32[1,128]{1,0:T(1,128)S(1)}) custom-call(f32[4,16,8,256]{3,2,1,0:T(8,128)} %grid_hbm.1, f32[4,16,8,256]{3,2,1,0:T(8,128)} %first_hbm.1, f32[4,16,8,256]{3,2,1,0:T(8,128)} %second_hbm.1, ...), custom_call_target="tpu_custom_call" | custom-call | tf_op jit(solution)/shard_map/render_step/pallas_call | solution.py:491
  18.1 1.2 %adam.1 = (f32[4,16,8,256]{3,2,1,0:T(8,128)}, f32[4,16,8,256]{3,2,1,0:T(8,128)}, f32[4,16,8,256]{3,2,1,0:T(8,128)}) custom-call(f32[4,16,8,256]{3,2,1,0:T(8,128)S(1)} %get-tuple-element.8.grid_ref, f32[4,16,8,256]{3,2,1,0:T(8,128)S(1)} %get-tuple-element.9.first_ref, f32[4,16,8,256]{3,2,1,0:T(8,128)S(1)} %get-tuple-element.10.second_ref, ...), custom_call_target="tpu_custom_call" | custom-call | tf_op jit(solution)/shard_map/adam/pallas_call | solution.py:540

commit v7 on v6

--- a/solution.py
+++ b/solution.py
@@ -21,6 +21,9 @@
 CHUNK = 512
 WIDTH = 256
 OPENING = 1
+FINE = jnp.float8_e4m3fn
+TABLE_SCALE = 65536.0
+COTANGENT_SCALE = 32.0
 PIECES = 4
 DIRECT_LIMIT = 64
 MESH = pl.DeviceIdType.MESH
@@ -31,7 +34,7 @@
     grid_hbm, first_hbm, second_hbm, pix_hbm, start_hbm, count_hbm, target_hbm,
     grid_ref, first_ref, second_ref, grad_ref, scale_ref,
     ints_ref, target_ref,
-    pair_ref, trans_ref, weight_ref, sig_ref, onehot_ref, row_ref, table_ref,
+    high_ref, low_ref, trans_ref, weight_ref, sig_ref, onehot_ref, row_ref, table_ref,
     whole_ref, wholes_ref, front_ref, own_ref, last_ref, far_ref,
     edge_ref, xhalo_ref, zhalo_ref, nsend_ref, nrecv_ref,
     whole_sem, part_send, part_recv, ready_sem, halo_send, halo_recv, norm_send, norm_recv, load_sem,
@@ -124,10 +127,10 @@
     for c in range(3):
         whole_ref[c] = sums[c]
     whole_ref[3] = before
-    full = table_ref[...]
+    full = TABLE_SCALE * table_ref[...]
     high = full.astype(jnp.bfloat16)
-    pair_ref[:, :ry] = high
-    pair_ref[:, ry:] = (full - high.astype(jnp.float32)).astype(jnp.bfloat16)
+    high_ref[...] = high
+    low_ref[...] = (full - high.astype(jnp.float32)).astype(FINE)
 
     def waiter(ref, sem):
         return pltpu.make_async_remote_copy(
@@ -199,16 +202,16 @@
                 length = jnp.where(slab >= start, length, 0)
                 row_ref[:, at] = jnp.where(length > 0, (length - 1) * rx + px, -1)
                 hot = jnp.where(y_ids == py, jnp.ones((), jnp.bfloat16), jnp.zeros((), jnp.bfloat16))
+                hot = hot.astype(FINE)
                 onehot_ref[:, at] = hot
                 for q in units:
-                    pltpu.matmul_push_rhs(hot[:, q * WIDTH:(q + 1) * WIDTH], j % 2, q)
-                for c in range(4):
-                    block = pl.ds(c * rows, rows)
                     for half in range(2):
-                        lhs = pair_ref[block, half * ry:(half + 1) * ry]
+                        pltpu.matmul_push_rhs(hot[:, q * WIDTH:(q + 1) * WIDTH], half, q)
+                for half, side in enumerate((high_ref, low_ref)):
+                    for c in range(4):
+                        lhs = side[pl.ds(c * rows, rows), :]
                         for q in units:
-                            fresh = j % 2 if c == 0 and half == 0 else None
-                            pltpu.matmul_acc_lhs(banks[j % 2][q][c], lhs, fresh)
+                            pltpu.matmul_acc_lhs(banks[j % 2][q][c], lhs, None if c else half)
             if j == 0:
                 continue
             i = j - 1
@@ -217,6 +220,7 @@
             for c in range(4):
                 u = jnp.concatenate([pltpu.matmul_pop(banks[i % 2][q][c]) for q in units], axis=1)
                 part = jnp.sum(jnp.where(mask, u, 0.0), axis=0, keepdims=True)
+                part = part * (1.0 / TABLE_SCALE)
                 if c == 3:
                     part = jnp.where(row < 0, 1.0, part)
                 own_ref[i, c] = part
@@ -311,7 +315,8 @@
 
         target_load.wait()
         for q in units:
-            pltpu.matmul_push_rhs(columns(0, q), 0, q, transpose=True)
+            for half in range(2):
+                pltpu.matmul_push_rhs(columns(0, q), half, q, transpose=True)
         for j in range(chunks):
             for n in range(1, reach + 1):
                 size = far_ref.shape[1] if n == reach else 4 * n
@@ -336,23 +341,25 @@
             pc = own_ref[j, pl.ds(0, 3), 0, :]
             pt = own_ref[j, 3]
             rendered = front_c + front_t * (pc + pt * beyond)
-            residual = RENDER_WEIGHT * (rendered - target_ref[:, at])
+            residual = (COTANGENT_SCALE * RENDER_WEIGHT) * (rendered - target_ref[:, at])
             color_cot = front_t * residual
             trans_cot = front_t * jnp.sum(residual * beyond, axis=0, keepdims=True)
             mask = row_ids16 == row_ref[:, at].astype(jnp.float32).astype(jnp.bfloat16)
-            for c in range(4):
-                cot = color_cot[c:c + 1] if c < 3 else trans_cot
-                top = cot.astype(jnp.bfloat16)
-                low = (cot - top.astype(jnp.float32)).astype(jnp.bfloat16)
-                for half, part in enumerate((top, low)):
-                    spread = jnp.where(mask, part, none)
+            cots = [color_cot[c:c + 1] for c in range(3)] + [trans_cot]
+            tops = [cot.astype(jnp.bfloat16) for cot in cots]
+            lows = [(cot - top.astype(jnp.float32)).astype(jnp.bfloat16) for cot, top in zip(cots, tops)]
+            for half, side in enumerate((tops, lows)):
+                for c in range(4):
+                    spread = jnp.where(mask, side[c], none)
+                    if half:
+                        spread = spread.astype(FINE)
                     for q in units:
-                        fresh = j % 2 if c == 0 and half == 0 else None
                         pltpu.matmul_acc_lhs(
-                            sums_acc[q][c], spread[:, q * WIDTH:(q + 1) * WIDTH], fresh)
+                            sums_acc[q][c], spread[:, q * WIDTH:(q + 1) * WIDTH], None if c else half)
             if j + 1 < chunks:
                 for q in units:
-                    pltpu.matmul_push_rhs(columns(j + 1, q), (j + 1) % 2, q, transpose=True)
+                    for half in range(2):
+                        pltpu.matmul_push_rhs(columns(j + 1, q), half, q, transpose=True)
             if j >= chunks - inner:
                 for c in range((j - chunks + inner) * channels // inner, (j + 1 - chunks + inner) * channels // inner):
                     smooth_planes(c, range(1, depth - 1))
@@ -360,7 +367,8 @@
         for c in range(channels):
             smooth_planes(c, (0, depth - 1) if depth > 1 else (0,))
         for c in range(4):
-            table_ref[pl.ds(c * rows, rows), :] = sum(pltpu.matmul_pop(sums_acc[q][c]) for q in units)
+            gathered = sum(pltpu.matmul_pop(sums_acc[q][c]) for q in units)
+            table_ref[pl.ds(c * rows, rows), :] = (1.0 / COTANGENT_SCALE) * gathered
 
     pl.run_scoped(scatter, *[
         pltpu.ACC(q)((rows, WIDTH), jnp.float32) for q in units for _ in range(4)
@@ -496,11 +504,12 @@
         scratch_shapes=[
             pltpu.VMEM((3, 1, rays), jnp.int32),
             pltpu.VMEM(target.shape, f32),
-            pltpu.VMEM((channels * rows, 2 * ry), jnp.bfloat16),
+            pltpu.VMEM((channels * rows, ry), jnp.bfloat16),
+            pltpu.VMEM((channels * rows, ry), FINE),
             pltpu.VMEM((depth, rx, ry), f32),
             pltpu.VMEM((depth, rx, ry), f32),
             pltpu.VMEM((channels, depth, rx, ry), f32),
-            pltpu.VMEM((ry, rays), jnp.bfloat16),
+            pltpu.VMEM((ry, rays), FINE),
             pltpu.VMEM((1, rays), jnp.int32),
             pltpu.VMEM((channels * rows, ry), f32),
             pltpu.VMEM((4, rx, ry), f32),

time: 19.5 us -> 19 us (0.974)
  Pallas kernels: 18.7 us -> 18.2 us
    pallas_call x1, Pallas kernels: 17.4 us -> 16.9 us  [per_device(): pl.pallas_call(functools.partial(kernel, ns, nt, chunk), out_shape=(cells...]
where the time goes in v7:
time: 19 us; the launch traced here: 18.8 us
  Pallas kernels  18.2 us (96%)
  between operations  0.64 us (3%)
    pallas_call x1, Pallas kernels, per_device(): pl.pallas_call(functools.partial(kernel, ns, nt, chunk), out_shape=(cells...  16.9 us
    pallas_call x1, Pallas kernels, per_device(): pl.pallas_call(adam_kernel, out_shape=(cells, cells, cells), in_specs=[vm...  1.21 us

profile of v7, /device:TPU:0, one launch (start us, length us, event | category | flops | bytes accessed | tf_op | source)
XLA Modules:
  0.0 18.8 jit_solution(2517426166040866976)
XLA Ops:
  0.6 16.9 %render_step.1 = (f32[4,16,8,256]{3,2,1,0:T(8,128)S(1)}, f32[4,16,8,256]{3,2,1,0:T(8,128)S(1)}, f32[4,16,8,256]{3,2,1,0:T(8,128)S(1)}, f32[4,16,8,256]{3,2,1,0:T(8,128)S(1)}, f32[1,128]{1,0:T(1,128)S(1)}) custom-call(f32[4,16,8,256]{3,2,1,0:T(8,128)} %grid_hbm.1, f32[4,16,8,256]{3,2,1,0:T(8,128)} %first_hbm.1, f32[4,16,8,256]{3,2,1,0:T(8,128)} %second_hbm.1, ...), custom_call_target="tpu_custom_call" | custom-call | tf_op jit(solution)/shard_map/render_step/pallas_call | solution.py:499
  17.6 1.2 %adam.1 = (f32[4,16,8,256]{3,2,1,0:T(8,128)}, f32[4,16,8,256]{3,2,1,0:T(8,128)}, f32[4,16,8,256]{3,2,1,0:T(8,128)}) custom-call(f32[4,16,8,256]{3,2,1,0:T(8,128)S(1)} %get-tuple-element.8.grid_ref, f32[4,16,8,256]{3,2,1,0:T(8,128)S(1)} %get-tuple-element.9.first_ref, f32[4,16,8,256]{3,2,1,0:T(8,128)S(1)} %get-tuple-element.10.second_ref, ...), custom_call_target="tpu_custom_call" | custom-call | tf_op jit(solution)/shard_map/adam/pallas_call | solution.py:549

commit v8 on v7

--- a/solution.py
+++ b/solution.py
@@ -34,7 +34,7 @@
     grid_hbm, first_hbm, second_hbm, pix_hbm, start_hbm, count_hbm, target_hbm,
     grid_ref, first_ref, second_ref, grad_ref, scale_ref,
     ints_ref, target_ref,
-    high_ref, low_ref, trans_ref, weight_ref, sig_ref, onehot_ref, row_ref, table_ref,
+    high_ref, low_ref, trans_ref, weight_ref, sig_ref, onehot_ref, row_ref, step_ref, table_ref,
     whole_ref, wholes_ref, front_ref, own_ref, last_ref, far_ref,
     edge_ref, xhalo_ref, zhalo_ref, nsend_ref, nrecv_ref,
     whole_sem, part_send, part_recv, ready_sem, halo_send, halo_recv, norm_send, norm_recv, load_sem,
@@ -59,7 +59,7 @@
     if direct(ns, nt):
         phases = [[
             {"slab": lax.rem(slab + k // nt, ns), "tile": lax.rem(tile + k % nt, nt)}
-            for k in range(1, ns * nt)
+            for k in [*range(nt, ns * nt), *range(1, nt)]
         ]]
         near = reach
     else:
@@ -72,19 +72,19 @@
 
     pieces = split(depth)
     step = depth // pieces
+    for i, a in enumerate((pix_hbm, start_hbm, count_hbm)):
+        pltpu.make_async_copy(a, ints_ref.at[i], load_sem.at[1]).start()
+    ints_load = pltpu.make_async_copy(ints_ref, ints_ref, load_sem.at[1])
     grid_load = pltpu.make_async_copy(grid_hbm, grid_ref, load_sem.at[0])
     for c in range(channels):
         for p in range(pieces):
             at = pl.ds(p * step, step)
             pltpu.make_async_copy(grid_hbm.at[c, at], grid_ref.at[c, at], load_sem.at[0]).start()
-    for i, a in enumerate((pix_hbm, start_hbm, count_hbm)):
-        pltpu.make_async_copy(a, ints_ref.at[i], load_sem.at[1]).start()
-    ints_load = pltpu.make_async_copy(ints_ref, ints_ref, load_sem.at[1])
     target_load = pltpu.make_async_copy(target_hbm, target_ref, load_sem.at[2])
     target_load.start()
     moment_loads = [
-        pltpu.make_async_copy(first_hbm, first_ref, load_sem.at[3]),
-        pltpu.make_async_copy(second_hbm, second_ref, load_sem.at[4]),
+        pltpu.make_async_copy(first_hbm, first_ref, load_sem.at[0]),
+        pltpu.make_async_copy(second_hbm, second_ref, load_sem.at[1]),
     ]
 
     barrier = pltpu.get_barrier_semaphore()
@@ -98,6 +98,22 @@
                 barrier, inc=1, device_id={"slab": slab + k}, device_id_type=MESH)
         greeters = greeters + inside(slab + k).astype(jnp.int32)
 
+    ints_load.wait()
+    y_ids = lax.broadcasted_iota(jnp.int32, (ry, chunk), 0).astype(jnp.float32).astype(jnp.bfloat16)
+    for j in range(chunks):
+        at = pl.ds(j * chunk, chunk)
+        pix = pix_ref[:, at]
+        start = start_ref[:, at]
+        px = pix // ry
+        py = (pix - px * ry).astype(jnp.float32).astype(jnp.bfloat16)
+        length = jnp.clip((start - slab) * depth + count_ref[:, at], 0, depth)
+        length = jnp.where(slab >= start, length, 0)
+        row_ref[:, at] = jnp.where(length > 0, (length - 1) * rx + px, -1)
+        step_ref[:, at] = (slab - start - 1) * rx + px
+        hot = jnp.where(y_ids == py, jnp.ones((), jnp.bfloat16), jnp.zeros((), jnp.bfloat16))
+        hot = hot.astype(FINE)
+        onehot_ref[:, at] = hot
+
     grid_load.wait()
     for copy in moment_loads:
         copy.start()
@@ -110,7 +126,7 @@
     for z in range(depth):
         s = grid_ref[0, z]
         e = jnp.exp(-jnp.abs(s))
-        tau = (jnp.maximum(s, 0.0) + jnp.log1p(e)) * span
+        tau = (jnp.maximum(s, 0.0) + jnp.log(1.0 + e)) * span
         sig_ref[0, z] = jnp.where(s >= 0, 1.0, e) / (1.0 + e)
         total = total + tau
         after = jnp.exp(-total)
@@ -171,13 +187,11 @@
         src = last_ref if k == reach else own_ref
         return pltpu.make_async_remote_copy(
             src_ref=src.at[j], dst_ref=far_ref.at[j, pl.ds(4 * (k - 1), src.shape[1])],
-            send_sem=part_send.at[k - 1], recv_sem=part_recv.at[j],
+            send_sem=part_send.at[k - 1], recv_sem=part_recv.at[lot_of(j, chunks)],
             device_id=slab_peer(ns - k), device_id_type=MESH)
 
-    y_ids = lax.broadcasted_iota(jnp.int32, (ry, chunk), 0).astype(jnp.float32).astype(jnp.bfloat16)
     row_ids = lax.broadcasted_iota(jnp.int32, (rows, chunk), 0)
 
-    ints_load.wait()
     units = range(chunk // WIDTH)
 
     def enter():
@@ -193,17 +207,7 @@
         banks = [[accs[(b * len(units) + q) * 4:][:4] for q in units] for b in range(2)]
         for j in range(chunks + 1):
             if j < chunks:
-                at = pl.ds(j * chunk, chunk)
-                pix = pix_ref[:, at]
-                start = start_ref[:, at]
-                px = pix // ry
-                py = (pix - px * ry).astype(jnp.float32).astype(jnp.bfloat16)
-                length = jnp.clip((start - slab) * depth + count_ref[:, at], 0, depth)
-                length = jnp.where(slab >= start, length, 0)
-                row_ref[:, at] = jnp.where(length > 0, (length - 1) * rx + px, -1)
-                hot = jnp.where(y_ids == py, jnp.ones((), jnp.bfloat16), jnp.zeros((), jnp.bfloat16))
-                hot = hot.astype(FINE)
-                onehot_ref[:, at] = hot
+                hot = onehot_ref[:, pl.ds(j * chunk, chunk)]
                 for q in units:
                     for half in range(2):
                         pltpu.matmul_push_rhs(hot[:, q * WIDTH:(q + 1) * WIDTH], half, q)
@@ -296,31 +300,36 @@
         def columns(j, q):
             return onehot_ref[:, pl.ds(j * chunk + q * WIDTH, WIDTH)]
 
-        for j in range(chunks):
-            at = pl.ds(j * chunk, chunk)
+        def front_start(j):
             for q in units:
-                pltpu.matmul_push_rhs(columns(j, q), j % 2, q)
+                pltpu.matmul_push_rhs(columns(j, q), 0, q)
             for half, lhs in enumerate((fold_high, fold_low)):
                 for q in units:
-                    pltpu.matmul_acc_lhs(steps[j % lags][q], lhs, None if half else j % 2)
-            behind = slab - start_ref[:, at]
-            mask = step_ids == (behind - 1) * rx + pix_ref[:, at] // ry
+                    pltpu.matmul_acc_lhs(steps[j % lags][q], lhs, None if half else 0)
+
+        def front_end(j):
+            at_step = step_ref[:, pl.ds(j * chunk, chunk)]
+            mask = step_ids == at_step
             u = jnp.concatenate([pltpu.matmul_pop(steps[j % lags][q]) for q in units], axis=1)
             for c in range(4):
                 picked = jnp.where(mask, u[c * step_rows:(c + 1) * step_rows], 0.0)
                 value = jnp.sum(picked, axis=0, keepdims=True)
                 if c == 3:
-                    value = jnp.where(behind <= 0, 1.0, value)
+                    value = jnp.where(at_step < 0, 1.0, value)
                 front_ref[j, pl.ds(c, 1), :] = value
 
+        for j in range(min(2, chunks)):
+            front_start(j)
+        for j in range(min(2, chunks)):
+            front_end(j)
+
         target_load.wait()
-        for q in units:
-            for half in range(2):
-                pltpu.matmul_push_rhs(columns(0, q), half, q, transpose=True)
         for j in range(chunks):
-            for n in range(1, reach + 1):
+            lot = [i for i in range(chunks) if lot_of(i, chunks) == lot_of(j, chunks)]
+            for n in range(1, reach + 1 if j == lot[0] else 0):
                 size = far_ref.shape[1] if n == reach else 4 * n
-                pl.when(ahead_count == n)(waiter(far_ref.at[j, pl.ds(0, size)], part_recv.at[j]).wait_recv)
+                part = far_ref.at[pl.ds(j, len(lot)), pl.ds(0, size)]
+                pl.when(ahead_count == n)(waiter(part, part_recv.at[lot_of(j, chunks)]).wait_recv)
             if j == chunks - inner:
                 wait_received(xhalo_ref, halo_recv.at[1], beside_count, 2)
             if j == 0 and direct(ns, nt):
@@ -330,6 +339,11 @@
                         pl.semaphore_signal(
                             ready_sem, inc=1, device_id={"slab": slab + k}, device_id_type=MESH)
             at = pl.ds(j * chunk, chunk)
+            if j + 2 < chunks:
+                front_start(j + 2)
+            for q in units:
+                for half in range(2):
+                    pltpu.matmul_push_rhs(columns(j, q), 1 - half, q, transpose=True)
             front_c = front_ref[j, pl.ds(0, 3), :]
             front_t = front_ref[j, pl.ds(3, 1), :]
             beyond = far_ref[j, pl.ds(4 * (reach - 1), 3), 0, :]
@@ -355,11 +369,9 @@
                         spread = spread.astype(FINE)
                     for q in units:
                         pltpu.matmul_acc_lhs(
-                            sums_acc[q][c], spread[:, q * WIDTH:(q + 1) * WIDTH], None if c else half)
-            if j + 1 < chunks:
-                for q in units:
-                    for half in range(2):
-                        pltpu.matmul_push_rhs(columns(j + 1, q), half, q, transpose=True)
+                            sums_acc[q][c], spread[:, q * WIDTH:(q + 1) * WIDTH], None if c else 1 - half)
+            if j + 2 < chunks:
+                front_end(j + 2)
             if j >= chunks - inner:
                 for c in range((j - chunks + inner) * channels // inner, (j + 1 - chunks + inner) * channels // inner):
                     smooth_planes(c, range(1, depth - 1))
@@ -398,7 +410,8 @@
         grad_ref[0, z] = out
         squares = squares + out * out
 
-    local = jnp.sum(squares)
+    lanes = jnp.sum(squares, axis=0, keepdims=True)
+    lanes = sum(lanes[:, i * 128:(i + 1) * 128] for i in range(ry // 128))
 
     def norm_copy(phase, slots, peer=None):
         src = nsend_ref.at[pl.ds(phase, 1)] if peer else nrecv_ref.at[slots]
@@ -410,7 +423,7 @@
     if direct(ns, nt):
         far = inside(slab - reach).astype(jnp.int32) + inside(slab + reach).astype(jnp.int32)
         pl.semaphore_wait(ready_sem, far)
-    value = jnp.full((1, 128), local, jnp.float32)
+    value = lanes
     base = 0
     for phase, peers in enumerate(phases):
         nsend_ref[phase] = value
@@ -431,7 +444,8 @@
         value = value + jnp.sum(nrecv_ref[pl.ds(base, len(peers)), 0, :], axis=0, keepdims=True)
         base += len(peers)
     limit = CLIP_RMS * math.sqrt(4.0 * total_depth * (rx * nt) * ry)
-    scale_ref[...] = limit / jnp.maximum(jnp.sqrt(value), limit)
+    total_square = jnp.sum(value, axis=1, keepdims=True)
+    scale_ref[...] = jnp.broadcast_to(limit / jnp.maximum(jnp.sqrt(total_square), limit), (1, 128))
     base = 0
     for phase, peers in enumerate(phases):
         norm_copy(phase, pl.ds(base, len(peers))).wait_send()
@@ -440,6 +454,10 @@
 
 def split(depth):
     return math.gcd(depth, PIECES)
+
+
+def lot_of(j, chunks):
+    return j // 2 if j < chunks - 1 else (chunks - 1) // 2 + 1
 
 
 def span_reach(ns):
@@ -511,6 +529,7 @@
             pltpu.VMEM((channels, depth, rx, ry), f32),
             pltpu.VMEM((ry, rays), FINE),
             pltpu.VMEM((1, rays), jnp.int32),
+            pltpu.VMEM((1, rays), jnp.int32),
             pltpu.VMEM((channels * rows, ry), f32),
             pltpu.VMEM((4, rx, ry), f32),
             pltpu.VMEM((reach, 4, rx, ry), f32),
@@ -525,13 +544,13 @@
             pltpu.VMEM((messages, 1, 128), f32),
             pltpu.SemaphoreType.DMA((2,)),
             pltpu.SemaphoreType.DMA((reach,)),
-            pltpu.SemaphoreType.DMA((chunks,)),
+            pltpu.SemaphoreType.DMA((lot_of(chunks - 1, chunks) + 1,)),
             pltpu.SemaphoreType.REGULAR,
             pltpu.SemaphoreType.DMA((2,)),
             pltpu.SemaphoreType.DMA((2,)),
             pltpu.SemaphoreType.DMA((phases,)),
             pltpu.SemaphoreType.DMA((phases,)),
-            pltpu.SemaphoreType.DMA((5,)),
+            pltpu.SemaphoreType.DMA((3,)),
         ],
         compiler_params=pltpu.CompilerParams(
             collective_id=0, has_side_effects=True, vmem_limit_bytes=32 * 1024 * 1024

time: 19 us -> 18.9 us (level)
  no operation moved by 1% of the time
where the time goes in v8:
time: 18.9 us; the launch traced here: 18.7 us
  Pallas kernels  18.1 us (96%)
  between operations  0.64 us (3%)
    pallas_call x1, Pallas kernels, per_device(): pl.pallas_call(functools.partial(kernel, ns, nt, chunk), out_shape=(cells...  16.9 us
    pallas_call x1, Pallas kernels, per_device(): pl.pallas_call(adam_kernel, out_shape=(cells, cells, cells), in_specs=[vm...  1.21 us

profile of v8, /device:TPU:0, one launch (start us, length us, event | category | flops | bytes accessed | tf_op | source)
XLA Modules:
  0.0 18.7 jit_solution(2825606334642272283)
XLA Ops:
  0.6 16.9 %render_step.1 = (f32[4,16,8,256]{3,2,1,0:T(8,128)S(1)}, f32[4,16,8,256]{3,2,1,0:T(8,128)S(1)}, f32[4,16,8,256]{3,2,1,0:T(8,128)S(1)}, f32[4,16,8,256]{3,2,1,0:T(8,128)S(1)}, f32[1,128]{1,0:T(1,128)S(1)}) custom-call(f32[4,16,8,256]{3,2,1,0:T(8,128)} %grid_hbm.1, f32[4,16,8,256]{3,2,1,0:T(8,128)} %first_hbm.1, f32[4,16,8,256]{3,2,1,0:T(8,128)} %second_hbm.1, ...), custom_call_target="tpu_custom_call" | custom-call | tf_op jit(solution)/shard_map/render_step/pallas_call | solution.py:517
  17.5 1.2 %adam.1 = (f32[4,16,8,256]{3,2,1,0:T(8,128)}, f32[4,16,8,256]{3,2,1,0:T(8,128)}, f32[4,16,8,256]{3,2,1,0:T(8,128)}) custom-call(f32[4,16,8,256]{3,2,1,0:T(8,128)S(1)} %get-tuple-element.8.grid_ref, f32[4,16,8,256]{3,2,1,0:T(8,128)S(1)} %get-tuple-element.9.first_ref, f32[4,16,8,256]{3,2,1,0:T(8,128)S(1)} %get-tuple-element.10.second_ref, ...), custom_call_target="tpu_custom_call" | custom-call | tf_op jit(solution)/shard_map/adam/pallas_call | solution.py:568

commit v9 on v8

--- a/solution.py
+++ b/solution.py
@@ -20,7 +20,6 @@
 EPSILON = 1e-08
 CHUNK = 512
 WIDTH = 256
-OPENING = 1
 FINE = jnp.float8_e4m3fn
 TABLE_SCALE = 65536.0
 COTANGENT_SCALE = 32.0
@@ -196,12 +195,12 @@
 
     def enter():
         pl.semaphore_wait(barrier, greeters)
+        for k in range(1, min(reach, ns - 1) + 1):
+            pl.when(slab == 0)(whole_copy(k).start)
         for k in range(reach, 0, -1):
-            pl.when(slab + k < ns)(whole_copy(k).start)
+            pl.when((slab > 0) & (slab + k < ns))(whole_copy(k).start)
         for copy, sends in halos[2:]:
             pl.when(sends)(copy.start)
-
-    opening = min(OPENING, chunks)
 
     def gather(*accs):
         banks = [[accs[(b * len(units) + q) * 4:][:4] for q in units] for b in range(2)]
@@ -211,7 +210,7 @@
                 for q in units:
                     for half in range(2):
                         pltpu.matmul_push_rhs(hot[:, q * WIDTH:(q + 1) * WIDTH], half, q)
-                for half, side in enumerate((high_ref, low_ref)):
+                for half, side in enumerate((low_ref, high_ref)):
                     for c in range(4):
                         lhs = side[pl.ds(c * rows, rows), :]
                         for q in units:
@@ -230,11 +229,12 @@
                 own_ref[i, c] = part
             for c in range(3):
                 last_ref[i, c] = own_ref[i, c] + BACKGROUND * part
-            if j < opening:
+            lot = [n for n in range(chunks) if lot_of(n, chunks) == lot_of(i, chunks)]
+            if i != lot[-1]:
                 continue
-            if j == opening:
+            if lot[0] == 0:
                 enter()
-            for n in range(0 if j == opening else i, j):
+            for n in lot:
                 for k in range(1, reach + 1):
                     pl.when(slab >= k)(part_copy(k, n).start)
 
@@ -271,6 +271,9 @@
             smooth = (g - below) + (g - above) + (g - left) + (g - right) + (g - down) + (g - up)
             grad_ref[c, z] = (2.0 * TV_WEIGHT) * smooth
 
+    wait_received(xhalo_ref, halo_recv.at[1], beside_count, 2)
+    for c in range(channels):
+        smooth_planes(c, range(1, depth - 1))
     wait_received(wholes_ref, whole_sem.at[1], behind_count, reach)
     folded = [[] for _ in range(4)]
     fold_t = jnp.ones((rx, ry), jnp.float32)
@@ -290,7 +293,6 @@
     row_ids16 = row_ids.astype(jnp.float32).astype(jnp.bfloat16)
     none = jnp.zeros((), jnp.bfloat16)
     lags = 4
-    inner = min(channels, chunks)
 
     def scatter(*accs):
         sums_acc = [accs[q * 4:][:4] for q in units]
@@ -330,8 +332,6 @@
                 size = far_ref.shape[1] if n == reach else 4 * n
                 part = far_ref.at[pl.ds(j, len(lot)), pl.ds(0, size)]
                 pl.when(ahead_count == n)(waiter(part, part_recv.at[lot_of(j, chunks)]).wait_recv)
-            if j == chunks - inner:
-                wait_received(xhalo_ref, halo_recv.at[1], beside_count, 2)
             if j == 0 and direct(ns, nt):
                 for k in (-reach, reach):
                     @pl.when(inside(slab + k))
@@ -372,9 +372,6 @@
                             sums_acc[q][c], spread[:, q * WIDTH:(q + 1) * WIDTH], None if c else 1 - half)
             if j + 2 < chunks:
                 front_end(j + 2)
-            if j >= chunks - inner:
-                for c in range((j - chunks + inner) * channels // inner, (j + 1 - chunks + inner) * channels // inner):
-                    smooth_planes(c, range(1, depth - 1))
         wait_received(zhalo_ref, halo_recv.at[0], level_count, 2)
         for c in range(channels):
             smooth_planes(c, (0, depth - 1) if depth > 1 else (0,))

time: 18.9 us -> 18.8 us (level)
  Pallas kernels: 18.1 us -> 17.9 us
where the time goes in v9:
time: 18.8 us; the launch traced here: 18.6 us
  Pallas kernels  17.9 us (95%)
  between operations  0.64 us (3%)
    pallas_call x1, Pallas kernels, per_device(): pl.pallas_call(functools.partial(kernel, ns, nt, chunk), out_shape=(cells...  16.7 us
    pallas_call x1, Pallas kernels, per_device(): pl.pallas_call(adam_kernel, out_shape=(cells, cells, cells), in_specs=[vm...  1.21 us

profile of v9, /device:TPU:0, one launch (start us, length us, event | category | flops | bytes accessed | tf_op | source)
XLA Modules:
  0.0 18.6 jit_solution(6186535735165784350)
XLA Ops:
  0.6 16.7 %render_step.1 = (f32[4,16,8,256]{3,2,1,0:T(8,128)S(1)}, f32[4,16,8,256]{3,2,1,0:T(8,128)S(1)}, f32[4,16,8,256]{3,2,1,0:T(8,128)S(1)}, f32[4,16,8,256]{3,2,1,0:T(8,128)S(1)}, f32[1,128]{1,0:T(1,128)S(1)}) custom-call(f32[4,16,8,256]{3,2,1,0:T(8,128)} %grid_hbm.1, f32[4,16,8,256]{3,2,1,0:T(8,128)} %first_hbm.1, f32[4,16,8,256]{3,2,1,0:T(8,128)} %second_hbm.1, ...), custom_call_target="tpu_custom_call" | custom-call | tf_op jit(solution)/shard_map/render_step/pallas_call | solution.py:514
  17.4 1.2 %adam.1 = (f32[4,16,8,256]{3,2,1,0:T(8,128)}, f32[4,16,8,256]{3,2,1,0:T(8,128)}, f32[4,16,8,256]{3,2,1,0:T(8,128)}) custom-call(f32[4,16,8,256]{3,2,1,0:T(8,128)S(1)} %get-tuple-element.8.grid_ref, f32[4,16,8,256]{3,2,1,0:T(8,128)S(1)} %get-tuple-element.9.first_ref, f32[4,16,8,256]{3,2,1,0:T(8,128)S(1)} %get-tuple-element.10.second_ref, ...), custom_call_target="tpu_custom_call" | custom-call | tf_op jit(solution)/shard_map/adam/pallas_call | solution.py:565

commit v10 on v9

--- a/solution.py
+++ b/solution.py
@@ -243,8 +243,7 @@
         for _ in range(2) for q in units for _ in range(4)
     ])
 
-    for copy, sends in halos[:2]:
-        pl.when(sends)(copy.start)
+    pl.when(halos[1][1])(halos[1][0].start)
     x_ids = lax.broadcasted_iota(jnp.int32, (rx, ry), 0)
     lane_ids = lax.broadcasted_iota(jnp.int32, (rx, ry), 1)
     first_x = tile == 0
@@ -274,6 +273,7 @@
     wait_received(xhalo_ref, halo_recv.at[1], beside_count, 2)
     for c in range(channels):
         smooth_planes(c, range(1, depth - 1))
+    pl.when(halos[0][1])(halos[0][0].start)
     wait_received(wholes_ref, whole_sem.at[1], behind_count, reach)
     folded = [[] for _ in range(4)]
     fold_t = jnp.ones((rx, ry), jnp.float32)
@@ -477,7 +477,7 @@
     linear = (1.0 - BETA_ONE) * scale
     square = (1.0 - BETA_TWO) * scale * scale
     pairs = ((first_out, first_hbm), (second_out, second_hbm), (grid_out, grid_hbm))
-    pieces = split(depth)
+    pieces = 2
     for c in range(channels):
         for p in range(pieces):
             planes = range(p * depth // pieces, (p + 1) * depth // pieces)

time: 18.8 us -> 18.9 us (level)
  no operation moved by 1% of the time
where the time goes in v10:
time: 18.9 us; the launch traced here: 18.7 us
  Pallas kernels  18 us (95%)
  between operations  0.64 us (3%)
    pallas_call x1, Pallas kernels, per_device(): pl.pallas_call(functools.partial(kernel, ns, nt, chunk), out_shape=(cells...  16.8 us
    pallas_call x1, Pallas kernels, per_device(): pl.pallas_call(adam_kernel, out_shape=(cells, cells, cells), in_specs=[vm...  1.23 us

profile of v10, /device:TPU:0, one launch (start us, length us, event | category | flops | bytes accessed | tf_op | source)
XLA Modules:
  0.0 18.7 jit_solution(13030909284718364037)
XLA Ops:
  0.6 16.8 %render_step.1 = (f32[4,16,8,256]{3,2,1,0:T(8,128)S(1)}, f32[4,16,8,256]{3,2,1,0:T(8,128)S(1)}, f32[4,16,8,256]{3,2,1,0:T(8,128)S(1)}, f32[4,16,8,256]{3,2,1,0:T(8,128)S(1)}, f32[1,128]{1,0:T(1,128)S(1)}) custom-call(f32[4,16,8,256]{3,2,1,0:T(8,128)} %grid_hbm.1, f32[4,16,8,256]{3,2,1,0:T(8,128)} %first_hbm.1, f32[4,16,8,256]{3,2,1,0:T(8,128)} %second_hbm.1, ...), custom_call_target="tpu_custom_call" | custom-call | tf_op jit(solution)/shard_map/render_step/pallas_call | solution.py:514
  17.4 1.2 %adam.1 = (f32[4,16,8,256]{3,2,1,0:T(8,128)}, f32[4,16,8,256]{3,2,1,0:T(8,128)}, f32[4,16,8,256]{3,2,1,0:T(8,128)}) custom-call(f32[4,16,8,256]{3,2,1,0:T(8,128)S(1)} %get-tuple-element.8.grid_ref, f32[4,16,8,256]{3,2,1,0:T(8,128)S(1)} %get-tuple-element.9.first_ref, f32[4,16,8,256]{3,2,1,0:T(8,128)S(1)} %get-tuple-element.10.second_ref, ...), custom_call_target="tpu_custom_call" | custom-call | tf_op jit(solution)/shard_map/adam/pallas_call | solution.py:565

commit v11 on v10

--- a/solution.py
+++ b/solution.py
@@ -71,6 +71,17 @@
 
     pieces = split(depth)
     step = depth // pieces
+    barrier = pltpu.get_barrier_semaphore()
+    greeters = nt - 1
+    for k in offsets:
+        @pl.when(inside(slab + k))
+        def _(k=k):
+            pl.semaphore_signal(
+                barrier, inc=1, device_id={"slab": slab + k}, device_id_type=MESH)
+        greeters = greeters + inside(slab + k).astype(jnp.int32)
+    for d in range(1, nt):
+        pl.semaphore_signal(barrier, inc=1, device_id=tile_peer(d), device_id_type=MESH)
+
     for i, a in enumerate((pix_hbm, start_hbm, count_hbm)):
         pltpu.make_async_copy(a, ints_ref.at[i], load_sem.at[1]).start()
     ints_load = pltpu.make_async_copy(ints_ref, ints_ref, load_sem.at[1])
@@ -85,17 +96,6 @@
         pltpu.make_async_copy(first_hbm, first_ref, load_sem.at[0]),
         pltpu.make_async_copy(second_hbm, second_ref, load_sem.at[1]),
     ]
-
-    barrier = pltpu.get_barrier_semaphore()
-    for d in range(1, nt):
-        pl.semaphore_signal(barrier, inc=1, device_id=tile_peer(d), device_id_type=MESH)
-    greeters = nt - 1
-    for k in offsets:
-        @pl.when(inside(slab + k))
-        def _(k=k):
-            pl.semaphore_signal(
-                barrier, inc=1, device_id={"slab": slab + k}, device_id_type=MESH)
-        greeters = greeters + inside(slab + k).astype(jnp.int32)
 
     ints_load.wait()
     y_ids = lax.broadcasted_iota(jnp.int32, (ry, chunk), 0).astype(jnp.float32).astype(jnp.bfloat16)
@@ -232,12 +232,11 @@
             lot = [n for n in range(chunks) if lot_of(n, chunks) == lot_of(i, chunks)]
             if i != lot[-1]:
                 continue
-            if lot[0] == 0:
-                enter()
             for n in lot:
                 for k in range(1, reach + 1):
                     pl.when(slab >= k)(part_copy(k, n).start)
 
+    enter()
     pl.run_scoped(gather, *[
         pltpu.ACC(q)((rows, WIDTH), jnp.float32)
         for _ in range(2) for q in units for _ in range(4)

time: 18.9 us -> 18.8 us (level)
  no operation moved by 1% of the time
where the time goes in v11:
time: 18.8 us; the launch traced here: 18.6 us
  Pallas kernels  18 us (96%)
  between operations  0.64 us (3%)
    pallas_call x1, Pallas kernels, per_device(): pl.pallas_call(functools.partial(kernel, ns, nt, chunk), out_shape=(cells...  16.8 us
    pallas_call x1, Pallas kernels, per_device(): pl.pallas_call(adam_kernel, out_shape=(cells, cells, cells), in_specs=[vm...  1.23 us

profile of v11, /device:TPU:0, one launch (start us, length us, event | category | flops | bytes accessed | tf_op | source)
XLA Modules:
  0.0 18.6 jit_solution(9736000106494250338)
XLA Ops:
  0.6 16.8 %render_step.1 = (f32[4,16,8,256]{3,2,1,0:T(8,128)S(1)}, f32[4,16,8,256]{3,2,1,0:T(8,128)S(1)}, f32[4,16,8,256]{3,2,1,0:T(8,128)S(1)}, f32[4,16,8,256]{3,2,1,0:T(8,128)S(1)}, f32[1,128]{1,0:T(1,128)S(1)}) custom-call(f32[4,16,8,256]{3,2,1,0:T(8,128)} %grid_hbm.1, f32[4,16,8,256]{3,2,1,0:T(8,128)} %first_hbm.1, f32[4,16,8,256]{3,2,1,0:T(8,128)} %second_hbm.1, ...), custom_call_target="tpu_custom_call" | custom-call | tf_op jit(solution)/shard_map/render_step/pallas_call | solution.py:513
  17.4 1.2 %adam.1 = (f32[4,16,8,256]{3,2,1,0:T(8,128)}, f32[4,16,8,256]{3,2,1,0:T(8,128)}, f32[4,16,8,256]{3,2,1,0:T(8,128)}) custom-call(f32[4,16,8,256]{3,2,1,0:T(8,128)S(1)} %get-tuple-element.8.grid_ref, f32[4,16,8,256]{3,2,1,0:T(8,128)S(1)} %get-tuple-element.9.first_ref, f32[4,16,8,256]{3,2,1,0:T(8,128)S(1)} %get-tuple-element.10.second_ref, ...), custom_call_target="tpu_custom_call" | custom-call | tf_op jit(solution)/shard_map/adam/pallas_call | solution.py:564
